TPU v7x, 256 devices: a whole 4x4x8 slice. The times are simulated.
256 devices in a mesh: seq: 16 (over y_lo, z), tensor: 16 (over y_hi, x, core).
Axes of the slice: x: 4, y: 4 (y_hi: 2, y_lo: 2; y = y_hi * 2 + y_lo), z: 8, core: 2. Of those that a mesh axis runs over, the one named last changes fastest.
Arguments:
- fixed_point: bfloat16 [2048, 4096], P(('seq', 'tensor')), may hold values from -6 to 6
- incoming: bfloat16 [2048, 4096], P(('seq', 'tensor')), may hold values from -6 to 6
- norm_gain: float32 [4096], replicated, may hold values from 0.1 to 1.9
- query_weight: bfloat16 [4096, 4096], P(None, 'tensor'), may hold values from -0.21875 to 0.21875, as said below
- key_weight: bfloat16 [4096, 4096], P(None, 'tensor'), may hold values from -0.265625 to 0.265625, as said below
- value_weight: bfloat16 [4096, 4096], P(None, 'tensor'), may hold values from -0.09375 to 0.09375
- out_weight: bfloat16 [4096, 4096], P('tensor'), may hold values from -0.09375 to 0.09375
- layout: int32 [32, 32], replicated, may hold values 0 or 1
Outputs:
- adjoint: float32 [2048, 4096], P(('seq', 'tensor'))
- gain_grad: float32 [4096], replicated
Inputs may be any that keep to these rules, and one draw needn't show every extreme that they name: `query_weight`: entries of the columns of each head are independent; their spread may differ between heads. `key_weight`: entries are independent within a draw; columns of some heads may follow the same head's columns of query_weight. `layout`: A key block strictly before a query block is attended where the entry at row query block, column key block is 1; a block always attends itself causally; entries on or above the diagonal are not read.
All inputs are finite; a program needn't handle non-finite values.
Results may differ from a plain program's by a relative error of at most 0.03.
Values may be sent and summed in bfloat16 or wider, within the bound.
A program may use at most 64 MiB of HBM per device.

v0:
```python
import functools

import jax
import jax.numpy as jnp
from jax import lax
from jax.sharding import Mesh
from jax.sharding import PartitionSpec as P

HEAD_DIM = 128
BLK = 64
ITERS = 2
TENSOR = ("tensor_0", "tensor_1", "tensor_2")
SEQ = ("seq_0", "seq_1")
SEQ_TENSOR = ("seq_0", "seq_1", "tensor_0", "tensor_1", "tensor_2")


EPS = 1e-05
THETA = 10000.0
MASKED = -1e30


def joined_along(blocks, dim):
    blocks = jnp.moveaxis(blocks, 0, dim)
    lengths = blocks.shape
    return blocks.reshape(*lengths[:dim], lengths[dim] * lengths[dim + 1], *lengths[dim + 2 :])


def sent_to_all(shard, axis):
    copies = jnp.broadcast_to(shard, (lax.axis_size(axis), *shard.shape))
    return lax.all_to_all(copies, axis, split_axis=0, concat_axis=0, tiled=True)


def gather_directly(shard, axis, dim):
    return joined_along(sent_to_all(shard, axis), dim)


def sent_together(arrays, axis, dim, along):
    ends, at = ([], 0)
    for a in arrays[:-1]:
        at += a.shape[along]
        ends.append(at)
    both = jnp.concatenate(arrays, axis=along)
    return tuple(jnp.split(lax.all_gather(both, axis, axis=dim, tiled=True), ends, axis=along))


def cut_along(shard, dim, devices):
    before, after = (shard.shape[:dim], shard.shape[dim + 1 :])
    return jnp.moveaxis(shard.reshape(*before, devices, -1, *after), dim, 0)


def sum_at_owner(shard, axis, dim):
    devices = lax.axis_size(axis)
    blocks = lax.all_to_all(cut_along(shard, dim, devices), axis, 0, 0, tiled=True)
    return jnp.sum(blocks.astype(jnp.float32), axis=0)


def one_axis_at_a_time(shard, axes):
    return functools.reduce(lax.psum, axes, shard)


def rope_tables(positions):
    freq = THETA ** (-jnp.arange(0, HEAD_DIM, 2, dtype=jnp.float32) / HEAD_DIM)
    angle = positions.astype(jnp.float32)[:, None] * freq[None, :]
    cosine = jnp.concatenate([jnp.cos(angle), jnp.cos(angle)], axis=1)[:, None, :]
    sine = jnp.concatenate([jnp.sin(angle), jnp.sin(angle)], axis=1)[:, None, :]
    return (cosine, sine)


def rotate(values, cosine, sine):
    half = HEAD_DIM // 2
    turned = jnp.concatenate([-values[..., half:], values[..., :half]], axis=-1)
    return values * cosine + turned * sine


def rotate_back(values, cosine, sine):
    half = HEAD_DIM // 2
    weighted = values * sine
    turned = jnp.concatenate([weighted[..., half:], -weighted[..., :half]], axis=-1)
    return values * cosine + turned


def expand_blocks(chosen):
    return jnp.repeat(jnp.repeat(chosen, BLK, axis=0), BLK, axis=1)


def pair_mask(query_pos, key_pos, chosen):
    query_block = (query_pos // BLK)[:, None]
    key_block = (key_pos // BLK)[None, :]
    earlier = (key_block < query_block) & chosen
    same = (key_block == query_block) & (key_pos[None, :] <= query_pos[:, None])
    return earlier | same


def body(
    fixed_point, incoming, norm_gain, query_weight, key_weight, value_weight, out_weight, layout
):
    local_rows, model_width = fixed_point.shape
    head_width = query_weight.shape[1]
    head_count = head_width // HEAD_DIM
    seq_tokens = local_rows * lax.axis_size(TENSOR)
    seq_length = seq_tokens * lax.axis_size(SEQ)
    seq_index = lax.axis_index(SEQ)
    score_scale = HEAD_DIM ** (-0.5)
    contract_last = (((1,), (1,)), ((), ()))
    head_shape = (seq_tokens, head_count, HEAD_DIM)
    point = fixed_point.astype(jnp.float32)
    inv_rms = lax.rsqrt(jnp.mean(point * point, axis=1, keepdims=True) + EPS)
    scaled = point * inv_rms
    normed = (norm_gain * scaled).astype(jnp.bfloat16)
    project_piece = gather_directly(normed, TENSOR, 0)
    projected = jnp.concatenate(
        [
            jnp.dot(project_piece, query_weight, preferred_element_type=jnp.float32),
            jnp.dot(project_piece, key_weight, preferred_element_type=jnp.float32),
            jnp.dot(project_piece, value_weight, preferred_element_type=jnp.float32),
        ],
        axis=1,
    )
    positions = seq_index * seq_tokens + jnp.arange(seq_tokens, dtype=jnp.int32)
    cosine, sine = rope_tables(positions)
    queries = rotate(projected[:, :head_width].reshape(head_shape), cosine, sine).astype(
        jnp.bfloat16
    )
    keys = rotate(
        projected[:, head_width : 2 * head_width].reshape(head_shape), cosine, sine
    ).astype(jnp.bfloat16)
    values = projected[:, 2 * head_width :].reshape(head_shape).astype(jnp.bfloat16)
    block_rows = seq_tokens // BLK
    block_count = seq_length // BLK
    first_block = seq_index * block_rows
    key_positions = jnp.arange(seq_length, dtype=jnp.int32)
    chosen_rows = (
        lax.dynamic_slice(layout, (first_block, jnp.int32(0)), (block_rows, block_count)) > 0
    )
    allowed = pair_mask(positions, key_positions, expand_blocks(chosen_rows))
    keys_all, values_all, queries_all = sent_together((keys, values, queries), SEQ, 0, 1)
    scores = (
        jnp.einsum("qhd,khd->hqk", queries, keys_all, preferred_element_type=jnp.float32)
        * score_scale
    )
    scores = jnp.where(allowed[None], scores, MASKED)
    log_norm = jax.nn.logsumexp(scores, axis=2, keepdims=True)
    probs = jnp.exp(scores - log_norm)
    probs_low = probs.astype(jnp.bfloat16)
    attended = jnp.einsum(
        "hqk,khd->qhd", probs_low, values_all, preferred_element_type=jnp.float32
    ).astype(jnp.bfloat16)
    attended_all = gather_directly(attended, SEQ, 0)
    log_all = gather_directly(log_norm[:, :, 0].T, SEQ, 0)
    chosen_cols = (
        lax.dynamic_slice(layout, (jnp.int32(0), first_block), (block_count, block_rows)) > 0
    )
    allowed_own = pair_mask(key_positions, positions, expand_blocks(chosen_cols))
    own_scores = (
        jnp.einsum("qhd,khd->hqk", queries_all, keys, preferred_element_type=jnp.float32)
        * score_scale
    )
    own_scores = jnp.where(allowed_own[None], own_scores, MASKED)
    own_probs = jnp.exp(own_scores - log_all.T[:, :, None])
    own_probs_low = own_probs.astype(jnp.bfloat16)
    cotangent = incoming.astype(jnp.float32)
    adjoint = cotangent
    gain_grad = jnp.zeros((model_width,), jnp.float32)
    for term_index in range(ITERS):
        grad_out = lax.dot_general(
            gather_directly(cotangent.astype(jnp.bfloat16), TENSOR, 0),
            out_weight,
            contract_last,
            preferred_element_type=jnp.float32,
        )
        grad_low = grad_out.astype(jnp.bfloat16).reshape(head_shape)
        delta = jnp.sum(grad_low.astype(jnp.float32) * attended.astype(jnp.float32), axis=2)
        grad_probs = jnp.einsum(
            "qhd,khd->hqk", grad_low, values_all, preferred_element_type=jnp.float32
        )
        grad_scores = (probs * (grad_probs - delta.T[:, :, None])).astype(jnp.bfloat16)
        grad_query = (
            jnp.einsum("hqk,khd->qhd", grad_scores, keys_all, preferred_element_type=jnp.float32)
            * score_scale
        )
        grad_all = gather_directly(grad_low, SEQ, 0)
        delta_all = jnp.sum(grad_all.astype(jnp.float32) * attended_all.astype(jnp.float32), axis=2)
        own_grad_probs = jnp.einsum(
            "qhd,khd->hqk", grad_all, values, preferred_element_type=jnp.float32
        )
        own_grad_scores = (own_probs * (own_grad_probs - delta_all.T[:, :, None])).astype(
            jnp.bfloat16
        )
        grad_key = (
            jnp.einsum(
                "hqk,qhd->khd", own_grad_scores, queries_all, preferred_element_type=jnp.float32
            )
            * score_scale
        )
        grad_value = jnp.einsum(
            "hqk,qhd->khd", own_probs_low, grad_all, preferred_element_type=jnp.float32
        )
        query_low = (
            rotate_back(grad_query, cosine, sine)
            .astype(jnp.bfloat16)
            .reshape(seq_tokens, head_width)
        )
        key_low = (
            rotate_back(grad_key, cosine, sine).astype(jnp.bfloat16).reshape(seq_tokens, head_width)
        )
        value_low = grad_value.astype(jnp.bfloat16).reshape(seq_tokens, head_width)
        total = lax.dot_general(
            query_low, query_weight, contract_last, preferred_element_type=jnp.float32
        )
        total = total + lax.dot_general(
            key_low, key_weight, contract_last, preferred_element_type=jnp.float32
        )
        total = total + lax.dot_general(
            value_low, value_weight, contract_last, preferred_element_type=jnp.float32
        )
        grad_normed = sum_at_owner(total.astype(jnp.bfloat16), TENSOR, 0)
        gain_term = jnp.sum(grad_normed * scaled, axis=0)
        gain_grad = gain_grad + one_axis_at_a_time(gain_term, SEQ_TENSOR)
        weighted = norm_gain * grad_normed
        inner = jnp.sum(weighted * scaled, axis=1, keepdims=True)
        cotangent = inv_rms * (weighted - scaled * (inner / model_width))
        adjoint = adjoint + cotangent
    return (adjoint, gain_grad * seq_length ** (-0.5))


def solution(mesh):
    split = Mesh(
        mesh.devices.reshape(2, 8, 2, 4, 2), ("seq_0", "seq_1", "tensor_0", "tensor_1", "tensor_2")
    )
    in_specs = (
        P(SEQ_TENSOR, None),
        P(SEQ_TENSOR, None),
        P(),
        P(None, TENSOR),
        P(None, TENSOR),
        P(None, TENSOR),
        P(TENSOR, None),
        P(),
    )
    out_specs = (P(SEQ_TENSOR, None), P())
    return jax.shard_map(body, mesh=split, in_specs=in_specs, out_specs=out_specs, check_vma=False)
```

profile of v0, /device:TPU:1, one launch (start us, length us, event | category | flops | bytes accessed | tf_op | source)
XLA Modules:
  0.0 385.7 jit_solution(5436890029493262179)
XLA Ops:
  7.2 1.1 fusion.71
  8.8 0.9 fusion.61
  9.7 1.1 broadcast_in_dim.50
  10.8 8.4 %all-to-all-start = ((bf16[16,8,4096]{2,1,0:T(8,128)(2,1)}), bf16[16,8,4096]{2,1,0:T(8,128)(2,1)S(1)}, u32[]{:S(2)}, u32[]{:S(2)}) async-start(bf16[16,8,4096]{2,1,0:T(8,128)(2,1)} %broadcast_in_dim.50), calls=%async_computation | async-start | bytes 2097152 | tf_op jit(solution)/shard_map/all_to_all | solution.py:30
  19.3 4.1 %copy.155 = bf16[256,4096]{1,0:T(8,128)(2,1)} copy(bf16[256,4096]{0,1:T(8,128)(2,1)} %bitcast.122) | data formatting | bytes 4194304 | tf_op jit(solution)/shard_map/dot_general | solution.py:115
  23.4 4.1 %copy.154 = bf16[256,4096]{1,0:T(8,128)(2,1)} copy(bf16[256,4096]{0,1:T(8,128)(2,1)} %bitcast.120) | data formatting | bytes 4194304 | tf_op jit(solution)/shard_map/dot_general | solution.py:114
  27.6 4.1 %copy.156 = bf16[256,4096]{1,0:T(8,128)(2,1)} copy(bf16[256,4096]{0,1:T(8,128)(2,1)} %bitcast.121) | data formatting | bytes 4194304 | tf_op jit(solution)/shard_map/dot_general | solution.py:113
  32.5 4.0 %all-to-all-done = bf16[16,8,4096]{2,1,0:T(8,128)(2,1)S(1)} async-done(((bf16[16,8,4096]{2,1,0:T(8,128)(2,1)}), bf16[16,8,4096]{2,1,0:T(8,128)(2,1)S(1)}, u32[]{:S(2)}, u32[]{:S(2)}) %all-to-all-start) | async-done | bytes 1048608 | tf_op jit(solution)/shard_map/all_to_all | solution.py:30
  36.5 2.4 fusion.35
  39.8 0.8 copy-done.9
  42.1 20.8 %all_to_all.45 = bf16[16,8,4096]{2,1,0:T(8,128)(2,1)S(1)} all-to-all(bf16[16,8,4096]{2,1,0:T(8,128)(2,1)S(1)} %broadcast_in_dim.95), channel_id=1, replica_groups=mesh['seq_0'=2,'seq_1'=8,'tensor_0'=2,'tensor_1'=4,'tensor_2'=2] {'tenso..., dimensions={0} | all-to-all | bytes 2097152 | tf_op jit(solution)/shard_map/all_to_all | solution.py:30
  62.9 0.8 convolution_convert_fusion.1
  63.8 1.2 broadcast_in_dim.102
  65.0 12.5 %all-to-all-start.3 = ((bf16[16,128,2,128]{3,1,2,0:T(8,128)(2,1)}), bf16[16,128,2,128]{3,1,2,0:T(8,128)(2,1)S(1)}, u32[]{:S(2)}, u32[]{:S(2)}) async-start(bf16[16,128,2,128]{3,1,2,0:T(8,128)(2,1)} %broadcast_in_dim.102), calls=%async_computation.3 | async-start | bytes 2097152 | tf_op jit(solution)/shard_map/all_to_all | solution.py:30
  78.6 1.2 fusion.45
  79.7 2.0 copy.120
  81.8 46.8 %all-gather.2.cloned.1.call-done = bf16[2048,6,128]{0,2,1:T(8,128)(2,1)} async-done(((bf16[128,6,128]{0,2,1:T(8,128)(2,1)}), bf16[2048,6,128]{0,2,1:T(8,128)(2,1)}) %all-gather.2.cloned.1.call-update) | async-done | bytes 3145744 | tf_op jit(solution)/shard_map/all_gather | solution.py:43
  128.6 2.0 fusion.93
  130.7 1.3 copy-done.3
  133.1 5.8 %all-to-all-start.2 = ((f32[16,128,2]{1,2,0:T(2,128)}), f32[16,128,2]{1,2,0:T(2,128)}, u32[]{:S(2)}, u32[]{:S(2)}) async-start(f32[16,128,2]{1,2,0:T(2,128)} %broadcast_in_dim.101), calls=%async_computation.2 | async-start | bytes 32768 | tf_op jit(solution)/shard_map/all_to_all | solution.py:30
  139.0 2.5 fusion.72
  141.6 4.8 %all-to-all-done.2 = f32[16,128,2]{1,2,0:T(2,128)} async-done(((f32[16,128,2]{1,2,0:T(2,128)}), f32[16,128,2]{1,2,0:T(2,128)}, u32[]{:S(2)}, u32[]{:S(2)}) %all-to-all-start.2) | async-done | bytes 16416 | tf_op jit(solution)/shard_map/all_to_all | solution.py:30
  146.4 1.2 broadcast_in_dim.103
  147.6 4.6 %all-to-all-start.4 = ((bf16[16,128,2,128]{3,1,2,0:T(8,128)(2,1)}), bf16[16,128,2,128]{3,1,2,0:T(8,128)(2,1)}, u32[]{:S(2)}, u32[]{:S(2)}) async-start(bf16[16,128,2,128]{3,1,2,0:T(8,128)(2,1)} %broadcast_in_dim.103), calls=%async_computation.4 | async-start | bytes 2097152 | tf_op jit(solution)/shard_map/all_to_all | solution.py:30
  152.6 1.1 fusion.47
  153.7 1.1 copy.127
  154.7 1.3 copy.131
  156.0 3.1 fusion.23
  159.1 2.2 fusion.6
  161.4 1.3 copy-done.1
  162.7 1.2 convolution_convert_fusion.5
  163.9 3.9 %all-to-all-done.4 = bf16[16,128,2,128]{3,1,2,0:T(8,128)(2,1)} async-done(((bf16[16,128,2,128]{3,1,2,0:T(8,128)(2,1)}), bf16[16,128,2,128]{3,1,2,0:T(8,128)(2,1)}, u32[]{:S(2)}, u32[]{:S(2)}) %all-to-all-start.4) | async-done | bytes 1048608 | tf_op jit(solution)/shard_map/all_to_all | solution.py:30
  167.8 2.2 fusion.16
  170.0 3.5 broadcast_multiply_fusion.2
  173.5 0.9 fusion.91
  174.4 0.9 fusion.92
  175.3 1.0 fusion.79
  176.3 2.5 fusion.94
  178.8 0.8 convolution_add_fusion.3
  180.4 0.8 fusion.3
  181.3 37.1 %all_to_all.46 = bf16[16,8,4096]{2,1,0:T(8,128)(2,1)S(1)} all-to-all(bf16[16,8,4096]{2,1,0:T(8,128)(2,1)S(1)} %fusion.3), channel_id=1, replica_groups=mesh['seq_0'=2,'seq_1'=8,'tensor_0'=2,'tensor_1'=4,'tensor_2'=2] {'tenso..., dimensions={0} | all-to-all | bytes 2097152 | tf_op jit(solution)/shard_map/all_to_all | solution.py:53
  219.8 20.6 %all_to_all.47 = bf16[16,8,4096]{2,1,0:T(8,128)(2,1)S(1)} all-to-all(bf16[16,8,4096]{2,1,0:T(8,128)(2,1)S(1)} %broadcast_in_dim.104), channel_id=1, replica_groups=mesh['seq_0'=2,'seq_1'=8,'tensor_0'=2,'tensor_1'=4,'tensor_2'=2] {'tenso..., dimensions={0} | all-to-all | bytes 2097152 | tf_op jit(solution)/shard_map/all_to_all | solution.py:30
  240.4 0.8 convolution_convert_fusion
  241.5 1.2 broadcast_in_dim.105
  242.7 4.6 %all-to-all-start.7 = ((bf16[16,128,2,128]{3,1,2,0:T(8,128)(2,1)}), bf16[16,128,2,128]{3,1,2,0:T(8,128)(2,1)}, u32[]{:S(2)}, u32[]{:S(2)}) async-start(bf16[16,128,2,128]{3,1,2,0:T(8,128)(2,1)} %broadcast_in_dim.105), calls=%async_computation.7 | async-start | bytes 2097152 | tf_op jit(solution)/shard_map/all_to_all | solution.py:30
  247.3 3.2 fusion.25
  250.5 21.6 %all-to-all-done.7 = bf16[16,128,2,128]{3,1,2,0:T(8,128)(2,1)} async-done(((bf16[16,128,2,128]{3,1,2,0:T(8,128)(2,1)}), bf16[16,128,2,128]{3,1,2,0:T(8,128)(2,1)}, u32[]{:S(2)}, u32[]{:S(2)}) %all-to-all-start.7) | async-done | bytes 1048608 | tf_op jit(solution)/shard_map/all_to_all | solution.py:30
  272.1 1.4 copy.139
  274.0 1.1 convolution_convert_fusion.4
  275.1 2.8 fusion.17
  277.9 3.4 broadcast_multiply_fusion
  281.3 0.9 fusion.89
  282.2 0.9 fusion.90
  283.1 1.0 fusion.81
  284.0 2.6 fusion.95
  286.6 0.8 convolution_add_fusion.1
  288.2 0.8 fusion.2
  289.1 23.4 %all_to_all.48 = bf16[16,8,4096]{2,1,0:T(8,128)(2,1)S(1)} all-to-all(bf16[16,8,4096]{2,1,0:T(8,128)(2,1)S(1)} %fusion.2), channel_id=1, replica_groups=mesh['seq_0'=2,'seq_1'=8,'tensor_0'=2,'tensor_1'=4,'tensor_2'=2] {'tenso..., dimensions={0} | all-to-all | bytes 2097152 | tf_op jit(solution)/shard_map/all_to_all | solution.py:53
  312.9 5.0 %psum.84 = f32[4096]{0:T(1024)S(1)} all-reduce(f32[4096]{0:T(1024)S(1)} %add.146), channel_id=1, replica_groups=mesh['seq_0'=2,'seq_1'=8,'tensor_0'=2,'tensor_1'=4,'tensor_2'=2] {'seq_0'}, use_global_device_ids=true, to_apply=%region_12.13 | all-reduce | flops 4096 | bytes 32768 | tf_op jit(solution)/shard_map/psum | solution.py:58
  317.9 21.9 %psum.83 = f32[4096]{0:T(1024)S(1)} all-reduce(f32[4096]{0:T(1024)S(1)} %psum.84), channel_id=1, replica_groups=mesh['seq_0'=2,'seq_1'=8,'tensor_0'=2,'tensor_1'=4,'tensor_2'=2] {'seq_1'}, use_global_device_ids=true, to_apply=%region_13.14 | all-reduce | flops 4096 | bytes 32768 | tf_op jit(solution)/shard_map/psum | solution.py:58
  339.7 8.1 %psum.82 = f32[4096]{0:T(1024)S(1)} all-reduce(f32[4096]{0:T(1024)S(1)} %psum.83), channel_id=1, replica_groups=mesh['seq_0'=2,'seq_1'=8,'tensor_0'=2,'tensor_1'=4,'tensor_2'=2] {'tenso..., use_global_device_ids=true, to_apply=%region_14.15 | all-reduce | flops 4096 | bytes 32768 | tf_op jit(solution)/shard_map/psum | solution.py:58
  347.8 11.2 %psum.81 = f32[4096]{0:T(1024)S(1)} all-reduce(f32[4096]{0:T(1024)S(1)} %psum.82), channel_id=1, replica_groups=mesh['seq_0'=2,'seq_1'=8,'tensor_0'=2,'tensor_1'=4,'tensor_2'=2] {'tenso..., use_global_device_ids=true, to_apply=%region_15.16 | all-reduce | flops 4096 | bytes 32768 | tf_op jit(solution)/shard_map/psum | solution.py:58
  359.1 18.4 %psum.80 = f32[4096]{0:T(1024)S(1)} all-reduce(f32[4096]{0:T(1024)S(1)} %psum.81), channel_id=1, replica_groups=mesh['seq_0'=2,'seq_1'=8,'tensor_0'=2,'tensor_1'=4,'tensor_2'=2] {'tenso..., use_global_device_ids=true, to_apply=%region_16.17 | all-reduce | flops 4096 | bytes 32768 | tf_op jit(solution)/shard_map/psum | solution.py:58
  378.1 0.8 fusion.68
  (112 shorter events, 11.0 us)
Async XLA Ops:
  7.2 55.8 %copy-start = (bf16[256,4096]{1,0:T(8,128)(2,1)S(1)}, bf16[256,4096]{1,0:T(8,128)(2,1)}, u32[]{:S(2)}) copy-start(bf16[256,4096]{1,0:T(8,128)(2,1)} %param.14) | copy-start | bytes 6291460
  8.3 0.5 copy-start.27
  10.8 25.7 %all-to-all-start = ((bf16[16,8,4096]{2,1,0:T(8,128)(2,1)}), bf16[16,8,4096]{2,1,0:T(8,128)(2,1)S(1)}, u32[]{:S(2)}, u32[]{:S(2)}) async-start(bf16[16,8,4096]{2,1,0:T(8,128)(2,1)} %broadcast_in_dim.50), calls=%async_computation | async-start | bytes 2097152 | tf_op jit(solution)/shard_map/all_to_all | solution.py:30
  19.3 109.4 %all-gather.2.cloned.1.call-start = ((), (), s32[]{:S(2)}) async-start(), calls=%async_computation.9 | async-start | bytes 3342336 | tf_op jit(solution)/shard_map/all_gather | solution.py:43
  32.5 137.4 %copy-start.12 = (f32[128,128]{0,1:T(8,128)}, f32[128,128]{0,1:T(8,128)S(1)}, u32[]{:S(2)}) copy-start(f32[128,128]{0,1:T(8,128)S(1)} %get-tuple-element.30) | copy-start | bytes 196612
  36.5 2.5 copy-start.10
  39.0 1.6 copy-start.9
  39.8 2.3 copy-start.19
  39.8 2.2 copy-start.17
  63.8 64.9 %copy-start.20 = (bf16[128,2,128]{0,2,1:T(8,128)(2,1)S(1)}, bf16[128,2,128]{0,2,1:T(8,128)(2,1)}, u32[]{:S(2)}) copy-start(bf16[128,2,128]{0,2,1:T(8,128)(2,1)} %copy-done.19) | copy-start | bytes 196612
  65.0 67.4 %all-to-all-start.3 = ((bf16[16,128,2,128]{3,1,2,0:T(8,128)(2,1)}), bf16[16,128,2,128]{3,1,2,0:T(8,128)(2,1)S(1)}, u32[]{:S(2)}, u32[]{:S(2)}) async-start(bf16[16,128,2,128]{3,1,2,0:T(8,128)(2,1)} %broadcast_in_dim.102), calls=%async_computation.3 | async-start | bytes 2097152 | tf_op jit(solution)/shard_map/all_to_all | solution.py:30
  78.5 1.2 copy-start.32
  78.5 1.2 copy-start.33
  130.6 1.4 copy-start.3
  132.4 23.6 %copy-start.25 = (f32[2,128]{1,0:T(2,128)}, f32[2,128]{1,0:T(2,128)S(1)}, u32[]{:S(2)}) copy-start(f32[2,128]{1,0:T(2,128)S(1)} %fusion.87) | copy-start | bytes 3076
  132.5 15.1 %copy-start.8 = (bf16[16,128,2,128]{3,1,2,0:T(8,128)(2,1)}, bf16[16,128,2,128]{3,1,2,0:T(8,128)(2,1)S(1)}, u32[]{:S(2)}) copy-start(bf16[16,128,2,128]{3,1,2,0:T(8,128)(2,1)S(1)} %all-to-all-done.3) | copy-start | bytes 3145732
  133.1 13.2 %all-to-all-start.2 = ((f32[16,128,2]{1,2,0:T(2,128)}), f32[16,128,2]{1,2,0:T(2,128)}, u32[]{:S(2)}, u32[]{:S(2)}) async-start(f32[16,128,2]{1,2,0:T(2,128)} %broadcast_in_dim.101), calls=%async_computation.2 | async-start | bytes 32768 | tf_op jit(solution)/shard_map/all_to_all | solution.py:30
  141.5 13.3 %copy-start.13 = (bf16[128,2,128]{0,2,1:T(8,128)(2,1)}, bf16[128,2,128]{0,2,1:T(8,128)(2,1)S(1)}, u32[]{:S(2)}) copy-start(bf16[128,2,128]{0,2,1:T(8,128)(2,1)S(1)} %get-tuple-element.37) | copy-start | bytes 196612
  147.6 4.7 %copy-start.24 = (s32[32,32]{1,0:T(8,128)S(1)}, s32[32,32]{1,0:T(8,128)}, u32[]{:S(2)}) copy-start(s32[32,32]{1,0:T(8,128)} %param.15) | copy-start | bytes 12292
  147.6 20.2 %all-to-all-start.4 = ((bf16[16,128,2,128]{3,1,2,0:T(8,128)(2,1)}), bf16[16,128,2,128]{3,1,2,0:T(8,128)(2,1)}, u32[]{:S(2)}, u32[]{:S(2)}) async-start(bf16[16,128,2,128]{3,1,2,0:T(8,128)(2,1)} %broadcast_in_dim.103), calls=%async_computation.4 | async-start | bytes 2097152 | tf_op jit(solution)/shard_map/all_to_all | solution.py:30
  161.4 1.3 copy-start.1
  170.0 5.3 %copy-start.15 = (f32[128,128]{0,1:T(8,128)S(1)}, f32[128,128]{0,1:T(8,128)}, u32[]{:S(2)}) copy-start(f32[128,128]{0,1:T(8,128)} %get-tuple-element.28) | copy-start | bytes 196612
  176.2 2.6 copy-start.4
  178.8 1.6 copy-start.6
  178.8 1.6 copy-start.21
  181.3 37.3 %copy-start.11 = (bf16[8,4096]{1,0:T(8,128)(2,1)S(1)}, bf16[8,4096]{1,0:T(8,128)(2,1)}, u32[]{:S(2)}) copy-start(bf16[8,4096]{1,0:T(8,128)(2,1)} %param.8) | copy-start | bytes 196612
  181.3 37.3 %copy-start.16 = (f32[4096]{0:T(1024)S(1)}, f32[4096]{0:T(1024)}, u32[]{:S(2)}) copy-start(f32[4096]{0:T(1024)} %param.10) | copy-start | bytes 49156
  181.3 37.3 %copy-start.28 = (f32[8]{0:T(128)S(1)}, f32[8]{0:T(128)}, u32[]{:S(2)}) copy-start(f32[8]{0:T(128)} %copy-done.27) | copy-start | bytes 100
  219.3 0.5 copy-start.30
  241.2 6.0 %copy-start.14 = (bf16[128,2,128]{0,2,1:T(8,128)(2,1)S(1)}, bf16[128,2,128]{0,2,1:T(8,128)(2,1)}, u32[]{:S(2)}) copy-start(bf16[128,2,128]{0,2,1:T(8,128)(2,1)} %copy-done.13) | copy-start | bytes 196612
  241.2 6.1 %copy-start.26 = (f32[2,128]{1,0:T(2,128)S(1)}, f32[2,128]{1,0:T(2,128)}, u32[]{:S(2)}) copy-start(f32[2,128]{1,0:T(2,128)} %copy-done.25) | copy-start | bytes 3076
  242.7 29.4 %all-to-all-start.7 = ((bf16[16,128,2,128]{3,1,2,0:T(8,128)(2,1)}), bf16[16,128,2,128]{3,1,2,0:T(8,128)(2,1)}, u32[]{:S(2)}, u32[]{:S(2)}) async-start(bf16[16,128,2,128]{3,1,2,0:T(8,128)(2,1)} %broadcast_in_dim.105), calls=%async_computation.7 | async-start | bytes 2097152 | tf_op jit(solution)/shard_map/all_to_all | solution.py:30
  272.1 1.9 copy-start.2
  284.0 2.6 copy-start.5
  286.6 1.6 copy-start.7
  286.6 1.6 copy-start.22
  289.1 23.6 %copy-start.29 = (f32[8]{0:T(128)S(1)}, f32[8]{0:T(128)}, u32[]{:S(2)}) copy-start(f32[8]{0:T(128)} %copy-done.27) | copy-start | bytes 100
  289.1 23.8 %copy-start.23 = (f32[4096]{0:T(1024)S(1)}, f32[4096]{0:T(1024)}, u32[]{:S(2)}) copy-start(f32[4096]{0:T(1024)} %get-tuple-element.4) | copy-start | bytes 49156
  289.1 89.0 %copy-start.18 = (bf16[8,4096]{1,0:T(8,128)(2,1)S(1)}, bf16[8,4096]{1,0:T(8,128)(2,1)}, u32[]{:S(2)}) copy-start(bf16[8,4096]{1,0:T(8,128)(2,1)} %param.9) | copy-start | bytes 196612
  289.1 89.0 %copy-start.31 = (f32[8]{0:T(128)S(1)}, f32[8]{0:T(128)}, u32[]{:S(2)}) copy-start(f32[8]{0:T(128)} %copy-done.30) | copy-start | bytes 100
Sparse Core Ops, SparseCore 0:
  42.1 86.4 all-gather.1
where the time goes:
time: 387 us; the launch traced here: 386 us
  blocking collectives  166 us (43%)
  waiting for transfers between devices  81.1 us (21%)
  matrix products  36.1 us (9%)
  starting transfers between devices  36 us (9%)
  local copies, waits for them, and re-layouts  31.1 us (8%)
  other arithmetic  20.2 us (5%)
  between operations  14.7 us (4%)
    psum x5, blocking collectives, one_axis_at_a_time(): return functools.reduce(lax.psum, axes, shard)  64.6 us
    all_to_all x2, blocking collectives, sum_at_owner(): lax.all_to_all(cut_along(shard, dim, devices), axis, 0, 0, tiled=True)  60.5 us
    all_gather x1, waiting for transfers between devices, sent_together(): lax.all_gather(both, axis, axis=dim, tiled=True)  46.8 us
    all_to_all x2, blocking collectives, sent_to_all(): return lax.all_to_all(copies, axis, split_axis=0, concat_axis=0, tiled=True)  41.4 us
    all_to_all x5, starting transfers between devices, sent_to_all(): return lax.all_to_all(copies, axis, split_axis=0, concat_axis=0, tiled=True)  36 us
    all_to_all x5, waiting for transfers between devices, sent_to_all(): return lax.all_to_all(copies, axis, split_axis=0, concat_axis=0, tiled=True)  34.3 us
  transfers between devices with their start and end apart: 6, of which 5 were waited for; matrix products, arithmetic and copies ran while one was open for 10% of the time, Pallas kernels for 0%

commit v1 on v0

v1 whole, which is shorter than its diff:
```python
import functools

import jax
import jax.numpy as jnp
from jax import lax
from jax.experimental import pallas as pl
from jax.experimental.pallas import tpu as pltpu
from jax.sharding import Mesh
from jax.sharding import PartitionSpec as P

HEAD_DIM = 128
BLK = 64
ITERS = 2
EPS = 1e-05
THETA = 10000.0
MASKED = -1e30
AXES = ("seq_0", "seq_1", "tensor_0", "tensor_1", "tensor_2")
TENSOR = ("tensor_0", "tensor_1", "tensor_2")
SEQ = ("seq_0", "seq_1")
SEQ_TENSOR = AXES
MESH = pl.DeviceIdType.MESH
F32, BF16 = jnp.float32, jnp.bfloat16

NY, NZ, NH, NX, NC = 2, 8, 2, 4, 2
CHIPS = NH * NX
ROWS = 8
CROWS = NC * ROWS
TOK = CHIPS * CROWS
PLANE = NZ * TOK
D = 4096
HALF = D // 2
HEADS_DEV = 2
WIDTH = HEADS_DEV * HEAD_DIM
NBLK = 32

CHIP_STEPS = ((0, 1), (0, 3), (1, 0), (0, 2), (1, 1), (1, 3), (1, 2))
SEQ_STEPS = tuple((a, b) for a in range(NY) for b in range(NZ) if (a, b) != (0, 0))
KV, QDO, OTHER, DO2, OTHER2 = range(5)

NN = (((1,), (0,)), ((), ()))
NT = (((1,), (1,)), ((), ()))


def dot(a, b, dims=NN):
    return lax.dot_general(a, b, dims, preferred_element_type=F32)


def kernel(
    point_ref, inc_ref, gain_ref, cos_ref, sin_ref, lay_ref, wq_hbm, wk_hbm, wv_hbm, wo_hbm,
    adj_ref, gg_ref,
    wq, wk, wv, wo, loc, sc16, in16, ir16, irl, agx, agi, agc,
    kv, qdo, oth, do2, oth2, st, bq, bk, pq, pk, att, dqkv, tot, totf, drv, rsrc, rrv, gn,
    inl, inr, adj16, adjr, gacc, gt, gs, gh,
    w_sem, ags, agr, fws, fwr, d2s, d2r, rgs, rgr, yxs, yxr, sts, str_, rss, rsr, gts, gtr, gss, gsr,
):
    yl, z, yh, x, c = (lax.axis_index(a) for a in AXES)
    chip = yh * NX + x
    s = yl * NZ + z
    scale = HEAD_DIM ** (-0.5)

    def dev(yl_=None, z_=None, yh_=None, x_=None, c_=None):
        pick = lambda a, b: a if b is None else b
        return (pick(yl, yl_), pick(z, z_), pick(yh, yh_), pick(x, x_), pick(c, c_))

    partner = dev(c_=1 - c)
    own_half = pl.ds(pl.multiple_of(c * HALF, HALF), HALF)
    far_half = pl.ds(pl.multiple_of((1 - c) * HALF, HALF), HALF)
    own_rows = pl.ds(pl.multiple_of(c * ROWS, ROWS), ROWS)
    far_rows = pl.ds(pl.multiple_of((1 - c) * ROWS, ROWS), ROWS)

    def remote(src, dst, ssem, rsem, to):
        return pltpu.make_async_remote_copy(
            src_ref=src, dst_ref=dst, send_sem=ssem, recv_sem=rsem, device_id=to, device_id_type=MESH
        )

    def chip_to(k):
        a, b = CHIP_STEPS[k]
        return lax.rem(yh + a, NH), lax.rem(x + b, NX)

    def chip_from(k):
        a, b = CHIP_STEPS[k]
        return lax.rem(yh + NH - a, NH) * NX + lax.rem(x + NX - b, NX)

    def seq_to(k):
        a, b = SEQ_STEPS[k]
        return lax.rem(yl + a, NY), lax.rem(z + b, NZ)

    def seq_from(k):
        a, b = SEQ_STEPS[k]
        return lax.rem(yl + NY - a, NY) * NZ + lax.rem(z + NZ - b, NZ)

    loads = [
        pltpu.make_async_copy(h, v, w_sem.at[i])
        for i, (h, v) in enumerate(((wq_hbm, wq), (wk_hbm, wk), (wv_hbm, wv), (wo_hbm, wo)))
    ]
    for cp in loads:
        cp.start()

    @pl.loop(0, NZ)
    def _(i):
        kv[i] = jnp.zeros((TOK, 2 * WIDTH), BF16)
        qdo[i] = jnp.zeros((TOK, 2 * WIDTH), BF16)
        do2[i] = jnp.zeros((TOK, WIDTH), BF16)

    bar = pltpu.get_barrier_semaphore()
    greet = [partner]
    for k in range(len(CHIP_STEPS)):
        a, b = chip_to(k)
        greet.append(dev(yh_=a, x_=b))
    for k in range(len(SEQ_STEPS)):
        a, b = seq_to(k)
        greet.append(dev(yl_=a, z_=b))
    for g in greet:
        pl.semaphore_signal(bar, inc=1, device_id=g, device_id_type=MESH)

    pt = point_ref[...].astype(F32)
    inv = lax.rsqrt(jnp.mean(pt * pt, axis=1, keepdims=True) + EPS)
    loc[0] = pt * inv
    loc[1] = inc_ref[...].astype(F32)
    irl[...] = jnp.broadcast_to(inv, (ROWS, 128))
    pl.semaphore_wait(bar, len(greet))

    swaps = [
        remote(loc.at[0, :, far_half], sc16.at[own_rows, :], d2s.at[0], d2r.at[0], partner),
        remote(loc.at[1, :, far_half], in16.at[own_rows, :], d2s.at[1], d2r.at[1], partner),
        remote(irl, ir16.at[own_rows, :], d2s.at[2], d2r.at[2], partner),
    ]
    for cp in swaps:
        cp.start()
    sc16[own_rows, :] = loc[0, :, own_half]
    in16[own_rows, :] = loc[1, :, own_half]
    ir16[own_rows, :] = irl[...]
    gain_half = gain_ref[:, own_half]
    for cp, buf in zip(swaps, (sc16, in16, ir16)):
        cp.wait_send()
    remote(loc.at[0, :, far_half], sc16.at[far_rows, :], d2s.at[0], d2r.at[0], partner).wait_recv()
    remote(loc.at[1, :, far_half], in16.at[far_rows, :], d2s.at[1], d2r.at[1], partner).wait_recv()
    remote(irl, ir16.at[far_rows, :], d2s.at[2], d2r.at[2], partner).wait_recv()

    def gather_sends(buf, g):
        mine = buf.at[chip, :, own_half]
        out = [remote(mine, mine, ags.at[g, 7], agr.at[g, 7], partner)]
        for k in range(7):
            a, b = chip_to(k)
            out.append(remote(mine, mine, ags.at[g, k], agr.at[g, k], dev(yh_=a, x_=b)))
        return out

    def gather_start(buf, g):
        for cp in gather_sends(buf, g):
            cp.start()

    def gather_finish(buf, g):
        forwards = []
        for k in range(7):
            slot = buf.at[chip_from(k), :, own_half]
            remote(slot, slot, ags.at[g, k], agr.at[g, k], partner).wait_recv()
            cp = remote(slot, slot, fws.at[g, k], fwr.at[g, k], partner)
            cp.start()
            forwards.append(cp)
        far = buf.at[chip, :, far_half]
        remote(far, far, ags.at[g, 7], agr.at[g, 7], partner).wait_recv()
        for k in range(7):
            far = buf.at[chip_from(k), :, far_half]
            remote(far, far, fws.at[g, k], fwr.at[g, k], partner).wait_recv()
        for cp in forwards + gather_sends(buf, g):
            cp.wait_send()

    agx[chip, :, own_half] = (gain_half * sc16[...]).astype(BF16)
    gather_start(agx, 0)
    agi[chip, :, own_half] = in16[...].astype(BF16)
    gather_start(agi, 1)

    row_tok = s * TOK + lax.broadcasted_iota(jnp.int32, (TOK, 1), 0)
    row_blk = row_tok // BLK
    blk_col = lax.broadcasted_iota(jnp.int32, (TOK, NBLK), 1)
    lay = lay_ref[...].astype(BF16)
    onehot = jnp.where(blk_col == row_blk, 1.0, 0.0).astype(BF16)
    chosen_q = jnp.where(blk_col < row_blk, dot(onehot, lay), 0.0).astype(BF16)
    chosen_k = jnp.where(blk_col > row_blk, dot(onehot, lay, NT), 0.0).astype(BF16)
    for part in range(2):
        plane = yl if part == 0 else 1 - yl
        col_blk = plane * (PLANE // BLK) + lax.broadcasted_iota(jnp.int32, (NBLK, PLANE), 1) // BLK
        spread = jnp.where(lax.broadcasted_iota(jnp.int32, (NBLK, PLANE), 0) == col_blk, 1.0, 0.0)
        spread = spread.astype(BF16)
        col_tok = plane * PLANE + lax.broadcasted_iota(jnp.int32, (1, PLANE), 1)
        same = row_blk == col_tok // BLK
        ok = (dot(chosen_q, spread) > 0.5) | (same & (col_tok <= row_tok))
        bq[part] = jnp.where(ok, 0.0, MASKED)
        ok = (dot(chosen_k, spread) > 0.5) | (same & (col_tok >= row_tok))
        bk[part] = jnp.where(ok, 0.0, MASKED)

    def turn(v, h, back=False):
        v = v[:, h * HEAD_DIM : (h + 1) * HEAD_DIM]
        turned = pltpu.roll(v, HEAD_DIM // 2, 1) * sin_ref[...]
        return v * cos_ref[...] - turned if back else v * cos_ref[...] + turned

    for cp in loads:
        cp.wait()
    gather_finish(agx, 0)

    feats = agx[...].reshape(TOK, D)
    key_f = dot(feats, wk[...])
    val_f = dot(feats, wv[...])
    for h in range(HEADS_DEV):
        kv[z, :, h * HEAD_DIM : (h + 1) * HEAD_DIM] = turn(key_f, h).astype(BF16)
    kv[z, :, WIDTH:] = val_f.astype(BF16)

    def depth(sgn):
        return NZ // 2 - c if sgn > 0 else NZ // 2 - 1 + c

    def wanted(stream, sgn, d, at):
        full = depth(sgn)
        near = d <= full
        if stream in (OTHER, OTHER2):
            return near if stream == OTHER else near & (yl == 0)
        origin = lax.rem(at - sgn * d + NZ, NZ)
        later = stream == KV
        if later == (sgn > 0):
            return near & ((at >= d) if sgn > 0 else (at + d <= NZ - 1))
        return near & ((origin + full >= NZ) if sgn > 0 else (origin < full))

    bufs = (kv, qdo, oth, do2, oth2)

    def hop(stream, sgn, d):
        block = bufs[stream].at[lax.rem(z - sgn * (d - 1) + NZ, NZ)]
        to = dev(z_=lax.rem(z + sgn + NZ, NZ))
        i = 0 if sgn > 0 else 1
        return remote(block, block, rgs.at[stream, i, d - 1], rgr.at[stream, i, d - 1], to)

    def send_hop(stream, sgn, d):
        @pl.when(wanted(stream, sgn, d, lax.rem(z + sgn + NZ, NZ)))
        def _():
            hop(stream, sgn, d).start()

    def sent_hop(stream, sgn, d):
        @pl.when(wanted(stream, sgn, d, lax.rem(z + sgn + NZ, NZ)))
        def _():
            hop(stream, sgn, d).wait_send()

    def take_hop(stream, sgn, d):
        @pl.when(wanted(stream, sgn, d, z))
        def _():
            block = bufs[stream].at[lax.rem(z - sgn * d + NZ, NZ)]
            i = 0 if sgn > 0 else 1
            to = dev(z_=lax.rem(z + sgn + NZ, NZ))
            remote(
                block, block, rgs.at[stream, i, d - 1], rgr.at[stream, i, d - 1], to
            ).wait_recv()

    def ring_start(stream):
        for sgn in (1, -1):
            send_hop(stream, sgn, 1)

    def ring_step(streams, d):
        for stream in streams:
            for sgn in (1, -1):
                take_hop(stream, sgn, d)
                if d < NZ // 2:
                    send_hop(stream, sgn, d + 1)

    def ring_sent(streams):
        for d in range(1, NZ // 2 + 1):
            for stream in streams:
                for sgn in (1, -1):
                    sent_hop(stream, sgn, d)

    across = dev(yl_=1 - yl)

    def cross(stream, i):
        dst = bufs[stream].at[z]
        return remote(dst, dst, yxs.at[i], yxr.at[i], across)

    def cross_from(src, stream, i):
        return remote(src.at[z], bufs[stream].at[z], yxs.at[i], yxr.at[i], across)

    @pl.when(yl == 0)
    def _():
        cross_from(kv, OTHER, 0).start()

    ring_start(KV)
    que_f = dot(feats, wq[...])
    for h in range(HEADS_DEV):
        qdo[z, :, h * HEAD_DIM : (h + 1) * HEAD_DIM] = turn(que_f, h).astype(BF16)
    gather_finish(agi, 1)
    qdo[z, :, WIDTH:] = dot(agi[...].reshape(TOK, D), wo[...], NT).astype(BF16)

    @pl.when(yl == 1)
    def _():
        cross_from(qdo, OTHER, 0).start()

    ring_start(QDO)
    cross(OTHER, 0).wait_recv()
    ring_start(OTHER)
    for d in range(1, NZ // 2 + 1):
        ring_step((KV, QDO, OTHER), d)

    def lanes(h, base=0):
        return pl.ds(base + h * HEAD_DIM, HEAD_DIM)

    def rows_of(buf, h, base=0):
        return buf[:, :, lanes(h, base)].reshape(PLANE, HEAD_DIM)

    def as_row(col):
        return jnp.transpose(jnp.broadcast_to(col, (TOK, TOK)))[0:1, :]

    def forward(parts):
        for h in range(HEADS_DEV):
            query = qdo[z, :, lanes(h)]
            top = None
            for i, buf in enumerate(parts):
                sc = dot(query, rows_of(buf, h), NT) * scale + bq[i]
                pq[h, i] = sc
                m = jnp.max(sc, axis=1, keepdims=True)
                top = m if top is None else jnp.maximum(top, m)
            total = None
            for i, buf in enumerate(parts):
                e = jnp.exp(pq[h, i] - top)
                pq[h, i] = e
                l = jnp.sum(e, axis=1, keepdims=True)
                total = l if total is None else total + l
            inv_total = 1.0 / total
            out = None
            for i, buf in enumerate(parts):
                p = pq[h, i] * inv_total
                pq[h, i] = p
                o = dot(p.astype(BF16), rows_of(buf, h, WIDTH))
                out = o if out is None else out + o
            out = out.astype(BF16)
            att[:, lanes(h)] = out
            grad = qdo[z, :, lanes(h, WIDTH)]
            st[0, s, pl.ds(h, 1), :] = as_row(top + jnp.log(total))
            st[0, s, pl.ds(2 + h, 1), :] = as_row(
                jnp.sum(grad.astype(F32) * out.astype(F32), axis=1, keepdims=True)
            )

    @pl.when(yl == 0)
    def _():
        forward((kv,))

    @pl.when(yl == 1)
    def _():
        forward((kv, oth))

    def stats_sends(it):
        out = []
        for k in range(len(SEQ_STEPS)):
            a, b = seq_to(k)
            mine = st.at[it, s]
            out.append(remote(mine, mine, sts.at[it, k], str_.at[it, k], dev(yl_=a, z_=b)))
        return out

    def stats_wait(it):
        for k in range(len(SEQ_STEPS)):
            slot = st.at[it, seq_from(k)]
            remote(slot, slot, sts.at[it, k], str_.at[it, k], partner).wait_recv()
        for cp in stats_sends(it):
            cp.wait_send()

    def own_grad(it, h):
        return qdo[z, :, lanes(h, WIDTH)] if it == 0 else do2[z, :, lanes(h)]

    def query_side(it, parts):
        for h in range(HEADS_DEV):
            grad = own_grad(it, h)
            delta = jnp.sum(
                grad.astype(F32) * att[:, lanes(h)].astype(F32), axis=1, keepdims=True
            )
            out = None
            for i, buf in enumerate(parts):
                gp = dot(grad, rows_of(buf, h, WIDTH), NT)
                gsc = (pq[h, i] * (gp - delta)).astype(BF16)
                o = dot(gsc, rows_of(buf, h))
                out = o if out is None else out + o
            out = jnp.concatenate([out] * HEADS_DEV, axis=1) * scale
            dqkv[0, :, lanes(h)] = turn(out, h, True).astype(BF16)

    def key_side(it, parts, planes):
        grads = ((qdo, WIDTH), (oth, WIDTH)) if it == 0 else ((do2, 0), (oth2, 0))
        for h in range(HEADS_DEV):
            key = kv[z, :, lanes(h)]
            value = kv[z, :, lanes(h, WIDTH)]
            gk, gv = None, None
            for i, buf in enumerate(parts):
                row = lambda n, r: jnp.concatenate(
                    [st[n, planes[i] * NZ + j, pl.ds(r, 1), :] for j in range(NZ)], axis=1
                )
                query = rows_of(buf, h)
                if it == 0:
                    p = jnp.exp(dot(key, query, NT) * scale + bk[i] - row(0, h))
                    pk[h, i] = p
                else:
                    p = pk[h, i]
                grad = rows_of(grads[i][0], h, grads[i][1])
                v = dot(p.astype(BF16), grad)
                gv = v if gv is None else gv + v
                gp = dot(value, grad, NT)
                gsc = (p * (gp - row(it, 2 + h))).astype(BF16)
                k = dot(gsc, query)
                gk = k if gk is None else gk + k
            gk = jnp.concatenate([gk] * HEADS_DEV, axis=1) * scale
            dqkv[1, :, lanes(h)] = turn(gk, h, True).astype(BF16)
            dqkv[2, :, lanes(h)] = gv.astype(BF16)

    def backward(it):
        @pl.when(yl == 0)
        def _():
            query_side(it, (kv,))

        @pl.when(yl == 1)
        def _():
            query_side(it, (kv, oth))

        stats_wait(it)

        @pl.when(yl == 0)
        def _():
            key_side(it, (qdo, oth), (yl, 1 - yl))

        @pl.when(yl == 1)
        def _():
            key_side(it, (qdo,), (yl,))

        dq, dk, dv = dqkv[0], dqkv[1], dqkv[2]
        step = 512

        def part_of(base, j):
            rows = pl.ds(pl.multiple_of(base + j * step, step), step)
            return (
                dot(dq, wq[rows, :], NT) + dot(dk, wk[rows, :], NT) + dot(dv, wv[rows, :], NT)
            )

        @pl.loop(0, HALF // step)
        def _(j):
            cols = pl.ds(pl.multiple_of(j * step, step), step)
            tot[it, :, :, cols] = (
                part_of((1 - c) * HALF, j).astype(BF16).reshape(CHIPS, CROWS, step)
            )

        give = remote(tot.at[it], drv.at[it], d2s.at[3 + it], d2r.at[3 + it], partner)
        give.start()

        @pl.loop(0, HALF // step)
        def _(j):
            cols = pl.ds(pl.multiple_of(j * step, step), step)
            totf[:, :, cols] = part_of(c * HALF, j).reshape(CHIPS, CROWS, step)

        give.wait_recv()
        sends = []
        for k in range(7):
            a, b = chip_to(k)
            other = a * NX + b
            rsrc[it, k] = (totf[other] + drv[it, other].astype(F32)).astype(BF16)
            cp = remote(
                rsrc.at[it, k], rrv.at[it, k], rss.at[it, k], rsr.at[it, k], dev(yh_=a, x_=b)
            )
            cp.start()
            sends.append(cp)
        gn[...] = totf[chip] + drv[it, chip].astype(F32)
        for k in range(7):
            sends[k].wait_recv()
            gn[...] += rrv[it, k].astype(F32)

        grad_normed = gn[...]
        scaled = sc16[...]
        term = jnp.sum(grad_normed * scaled, axis=0, keepdims=True)
        gacc[...] = term if it == 0 else gacc[...] + term
        weighted = gain_half * grad_normed
        inl[it] = jnp.broadcast_to(
            jnp.sum(weighted * scaled, axis=1, keepdims=True), (CROWS, 128)
        )
        share = remote(inl.at[it], inr.at[it], d2s.at[5 + it], d2r.at[5 + it], partner)
        share.start()
        share.wait_recv()
        inner = (inl[it] + inr[it])[:, 0:1]
        cot = ir16[:, 0:1] * (weighted - scaled * (inner / D))
        adj16[...] = (in16[...] if it == 0 else adj16[...]) + cot
        give.wait_send()
        share.wait_send()
        for cp in sends:
            cp.wait_send()
        return cot

    for cp in stats_sends(0):
        cp.start()
    cot = backward(0)

    agc[chip, :, own_half] = cot.astype(BF16)
    gather_start(agc, 2)
    ring_sent((KV, QDO, OTHER))
    cross(OTHER, 0).wait_send()
    gather_finish(agc, 2)
    do2[z] = dot(agc[...].reshape(TOK, D), wo[...], NT).astype(BF16)

    @pl.when(yl == 1)
    def _():
        cross_from(do2, OTHER2, 1).start()

    ring_start(DO2)
    for h in range(HEADS_DEV):
        st[1, s, pl.ds(2 + h, 1), :] = as_row(
            jnp.sum(
                do2[z, :, lanes(h)].astype(F32) * att[:, lanes(h)].astype(F32),
                axis=1,
                keepdims=True,
            )
        )
    for cp in stats_sends(1):
        cp.start()

    @pl.when(yl == 0)
    def _():
        cross(OTHER2, 1).wait_recv()

    ring_start(OTHER2)
    for d in range(1, NZ // 2 + 1):
        ring_step((DO2, OTHER2), d)
    backward(1)

    back = remote(adj16.at[far_rows, :], adjr, d2s.at[7], d2r.at[7], partner)
    back.start()
    gt[chip] = gacc[...]
    sends = []
    for k in range(7):
        a, b = chip_to(k)
        cp = remote(gt.at[chip], gt.at[chip], gts.at[k], gtr.at[k], dev(yh_=a, x_=b))
        cp.start()
        sends.append(cp)
    for k in range(7):
        slot = gt.at[chip_from(k)]
        remote(slot, slot, gts.at[k], gtr.at[k], partner).wait_recv()
    acc = gt[0]
    for i in range(1, CHIPS):
        acc = acc + gt[i]
    gs[s] = acc
    for k in range(len(SEQ_STEPS)):
        a, b = seq_to(k)
        cp = remote(gs.at[s], gs.at[s], gss.at[k], gsr.at[k], dev(yl_=a, z_=b))
        cp.start()
        sends.append(cp)
    adj_ref[:, own_half] = adj16[own_rows, :]
    back.wait_recv()
    adj_ref[:, far_half] = adjr[...]
    for k in range(len(SEQ_STEPS)):
        slot = gs.at[seq_from(k)]
        remote(slot, slot, gss.at[k], gsr.at[k], partner).wait_recv()
    acc = gs[0]
    for i in range(1, NY * NZ):
        acc = acc + gs[i]
    gh[0] = acc * (NY * NZ * TOK) ** (-0.5)
    last = remote(gh.at[0], gh.at[1], d2s.at[8], d2r.at[8], partner)
    last.start()
    gg_ref[:, own_half] = gh[0]
    last.wait_recv()
    gg_ref[:, far_half] = gh[1]

    ring_sent((DO2, OTHER2))

    @pl.when(yl == 1)
    def _():
        cross_from(do2, OTHER2, 1).wait_send()

    for cp in sends + [back, last]:
        cp.wait_send()


def scratch():
    v = pltpu.VMEM
    dma = pltpu.SemaphoreType.DMA
    return [
        v((D, WIDTH), BF16), v((D, WIDTH), BF16), v((D, WIDTH), BF16), v((WIDTH, D), BF16),
        v((2, ROWS, D), F32), v((CROWS, HALF), F32), v((CROWS, HALF), F32), v((CROWS, 128), F32),
        v((ROWS, 128), F32),
        v((CHIPS, CROWS, D), BF16), v((CHIPS, CROWS, D), BF16), v((CHIPS, CROWS, D), BF16),
        v((NZ, TOK, 2 * WIDTH), BF16), v((NZ, TOK, 2 * WIDTH), BF16), v((NZ, TOK, 2 * WIDTH), BF16),
        v((NZ, TOK, WIDTH), BF16), v((NZ, TOK, WIDTH), BF16),
        v((ITERS, NY * NZ, 8, TOK), F32),
        v((2, TOK, PLANE), F32), v((2, TOK, PLANE), F32),
        v((HEADS_DEV, 2, TOK, PLANE), F32), v((HEADS_DEV, 2, TOK, PLANE), F32),
        v((TOK, WIDTH), BF16), v((3, TOK, WIDTH), BF16),
        v((ITERS, CHIPS, CROWS, HALF), BF16), v((CHIPS, CROWS, HALF), F32),
        v((ITERS, CHIPS, CROWS, HALF), BF16), v((ITERS, 7, CROWS, HALF), BF16),
        v((ITERS, 7, CROWS, HALF), BF16), v((CROWS, HALF), F32),
        v((ITERS, CROWS, 128), F32), v((ITERS, CROWS, 128), F32),
        v((CROWS, HALF), F32), v((ROWS, HALF), F32), v((1, HALF), F32),
        v((CHIPS, 1, HALF), F32), v((NY * NZ, 1, HALF), F32), v((2, 1, HALF), F32),
        dma((4,)), dma((3, 8)), dma((3, 8)), dma((3, 7)), dma((3, 7)), dma((9,)), dma((9,)),
        dma((5, 2, 4)), dma((5, 2, 4)), dma((2,)), dma((2,)),
        dma((ITERS, 15)), dma((ITERS, 15)), dma((ITERS, 7)), dma((ITERS, 7)),
        dma((7,)), dma((7,)), dma((15,)), dma((15,)),
    ]


def body(
    fixed_point, incoming, norm_gain, query_weight, key_weight, value_weight, out_weight, layout
):
    seq_index = lax.axis_index(SEQ)
    positions = (seq_index * TOK + jnp.arange(TOK, dtype=jnp.int32)).astype(F32)
    freq = THETA ** (-jnp.arange(0, HEAD_DIM, 2, dtype=F32) / HEAD_DIM)
    angle = positions[:, None] * freq[None, :]
    cosine = jnp.concatenate([jnp.cos(angle), jnp.cos(angle)], axis=1)
    sine = jnp.concatenate([-jnp.sin(angle), jnp.sin(angle)], axis=1)
    vmem = pl.BlockSpec(memory_space=pltpu.VMEM)
    hbm = pl.BlockSpec(memory_space=pl.ANY)
    adjoint, gain = pl.pallas_call(
        kernel,
        out_shape=(
            jax.ShapeDtypeStruct((ROWS, D), F32),
            jax.ShapeDtypeStruct((1, D), F32),
        ),
        in_specs=[vmem] * 6 + [hbm] * 4,
        out_specs=(vmem, vmem),
        scratch_shapes=scratch(),
        compiler_params=pltpu.CompilerParams(
            collective_id=0, has_side_effects=True, vmem_limit_bytes=60 * 1024 * 1024
        ),
        name="deq_backward",
    )(
        fixed_point, incoming, norm_gain[None, :], cosine, sine, (layout > 0).astype(F32),
        query_weight, key_weight, value_weight, out_weight,
    )
    return adjoint, gain[0]


def solution(mesh):
    split = Mesh(mesh.devices.reshape(NY, NZ, NH, NX, NC), AXES)
    in_specs = (
        P(SEQ_TENSOR, None),
        P(SEQ_TENSOR, None),
        P(),
        P(None, TENSOR),
        P(None, TENSOR),
        P(None, TENSOR),
        P(TENSOR, None),
        P(),
    )
    out_specs = (P(SEQ_TENSOR, None), P())
    return jax.shard_map(body, mesh=split, in_specs=in_specs, out_specs=out_specs, check_vma=False)
```

time: 387 us -> 147 us (0.38)
  blocking collectives: 166 us -> 0 us
  Pallas kernels: 0 us -> 140 us
  waiting for transfers between devices: 81.1 us -> 0 us
  matrix products: 36.1 us -> 0 us
  starting transfers between devices: 36 us -> 0 us
  local copies, waits for them, and re-layouts: 31.1 us -> 2.89 us
  other arithmetic: 20.2 us -> 2.4 us
  between operations: 14.7 us -> 0.66 us
    pallas_call x0 -> x1, Pallas kernels: none -> 140 us  [body(): pl.pallas_call(kernel, out_shape=(jax.ShapeDtypeStruct((ROWS, D), F32), j...]
    all_to_all x4 -> x0, blocking collectives: 102 us -> none  [the longest x2 60.5 us: sum_at_owner(): lax.all_to_all(cut_along(shard, dim, devices), axis, 0, 0, tiled=True)]
    psum x5 -> x0, blocking collectives: 64.6 us -> none  [one_axis_at_a_time(): return functools.reduce(lax.psum, axes, shard)]
    all_gather x1 -> x0, waiting for transfers between devices: 46.8 us -> none  [sent_together(): lax.all_gather(both, axis, axis=dim, tiled=True)]
    dot_general x20 -> x0, matrix products: 36.1 us -> none  [the longest x2 6.93 us: body(): jnp.einsum('hqk,qhd->khd', own_grad_scores, queries_all, preferred_elemen...]
    all_to_all x5 -> x0, starting transfers between devices: 36 us -> none  [sent_to_all(): return lax.all_to_all(copies, axis, split_axis=0, concat_axis=0, tiled=True)]
    all_to_all x5 -> x0, waiting for transfers between devices: 34.3 us -> none  [sent_to_all(): return lax.all_to_all(copies, axis, split_axis=0, concat_axis=0, tiled=True)]
    dot_general x3 -> x0, local copies, waits for them, and re-layouts: 12.4 us -> none  [the longest x1 4.13 us: body(): jnp.dot(project_piece, value_weight, preferred_element_type=jnp.float32)]
  transfers between devices with their start and end apart: 6 -> 0, of which waited for: 5 -> 0; matrix products, arithmetic and copies ran while one was open for 10% -> 0% of each run, Pallas kernels for 0% -> 0%
where the time goes in v1:
time: 147 us; the launch traced here: 146 us
  Pallas kernels  140 us (95%)
  local copies, waits for them, and re-layouts  2.89 us (2%)
  other arithmetic  2.4 us (2%)
    pallas_call x1, Pallas kernels, body(): pl.pallas_call(kernel, out_shape=(jax.ShapeDtypeStruct((ROWS, D), F32), j...  140 us

profile of v1, /device:TPU:1, one launch (start us, length us, event | category | flops | bytes accessed | tf_op | source)
XLA Modules:
  0.0 146.4 jit_solution(16956081971836310743)
XLA Ops:
  0.7 0.3 fusion
  1.0 0.8 pad_maximum_fusion
  1.7 1.3 compare_convert_fusion.lay_ref
  3.1 140.4 %deq_backward.1 = (f32[8,4096]{1,0:T(8,128)}, f32[1,4096]{1,0:T(1,128)}) custom-call(bf16[8,4096]{1,0:T(8,128)(2,1)} %point_ref.1, bf16[8,4096]{1,0:T(8,128)(2,1)} %inc_ref.1, f32[1,4096]{1,0:T(1,128)} %bitcast.2, f32[128,128]{1,0:T(8,128)} %get-tuple-element.9.cos_ref, f32[128,128]{1,0:T(8,128)} %get-tuple-element.10.sin_ref, ...), custom_call_target="tpu_custom_call" | custom-call | tf_op jit(solution)/shard_map/deq_backward/pallas_call | solution.py:604
  143.5 1.6 %copy.12 = f32[8,4096]{1,0:T(8,128)} copy(f32[8,4096]{1,0:T(8,128)} %get-tuple-element.13) | data formatting | bytes 262144
  145.1 1.3 copy.13
  (2 shorter events, 0.0 us)

commit v2 on v1

v2 whole, which is shorter than its diff:
```python
import functools

import jax
import jax.numpy as jnp
from jax import lax
from jax.experimental import pallas as pl
from jax.experimental.pallas import tpu as pltpu
from jax.sharding import Mesh
from jax.sharding import PartitionSpec as P

HEAD_DIM = 128
BLK = 64
ITERS = 2
EPS = 1e-05
THETA = 10000.0
MASKED = -1e30
AXES = ("seq_0", "seq_1", "tensor_0", "tensor_1", "tensor_2")
TENSOR = ("tensor_0", "tensor_1", "tensor_2")
SEQ = ("seq_0", "seq_1")
SEQ_TENSOR = AXES
MESH = pl.DeviceIdType.MESH
F32, BF16 = jnp.float32, jnp.bfloat16

NY, NZ, NH, NX, NC = 2, 8, 2, 4, 2
CHIPS = NH * NX
ROWS = 8
CROWS = NC * ROWS
TOK = CHIPS * CROWS
PLANE = NZ * TOK
D = 4096
HALF = D // 2
HEADS_DEV = 2
WIDTH = HEADS_DEV * HEAD_DIM
NBLK = 32

CHIP_STEPS = ((1, 2), (1, 1), (1, 3), (0, 2), (1, 0), (0, 1), (0, 3))
SEQ_STEPS = tuple(
    (a, b % NZ) for b in (4, 3, -3, 2, -2, 1, -1, 0) for a in (1, 0) if (a, b) != (0, 0)
)
K, V, Q, G, OA, GA, GB, OA2 = range(8)
CHUNKS = 2

NN = (((1,), (0,)), ((), ()))
NT = (((1,), (1,)), ((), ()))


def dot(a, b, dims=NN):
    return lax.dot_general(a, b, dims, preferred_element_type=F32)


def kernel(
    point_ref, inc_ref, gain_ref, freq_ref, lay_ref, wq_hbm, wk_hbm, wv_hbm, wo_hbm,
    adj_ref, gg_ref,
    wqkv, wo, wqkv_t, wo_t, cosb, sinb, loc, sc16, in16, ir16, irl, agx, agi, agc,
    kb, vb, qb, gb, oa, ob, ga2, gb2, oa2, ob2, st, bq, bk, pq, pk, att, dqkv,
    tot, drv, rsrc, rrv, pair, gn, inl, inr, adj16, adjr, gacc, gt, gs, gh,
    w_sem, ags, agr, fws, fwr, d2s, d2r, rgs, rgr, yxs, yxr, yfs, yfr, sts, str_,
    gvs, gvr, rss, rsr, gts, gtr, gss, gsr,
):
    yl, z, yh, x, c = (lax.axis_index(a) for a in AXES)
    chip = yh * NX + x
    s = yl * NZ + z
    scale = HEAD_DIM ** (-0.5)

    def dev(yl_=None, z_=None, yh_=None, x_=None, c_=None):
        pick = lambda a, b: a if b is None else b
        return (pick(yl, yl_), pick(z, z_), pick(yh, yh_), pick(x, x_), pick(c, c_))

    partner = dev(c_=1 - c)
    own_half = pl.ds(pl.multiple_of(c * HALF, HALF), HALF)
    far_half = pl.ds(pl.multiple_of((1 - c) * HALF, HALF), HALF)
    own_rows = pl.ds(pl.multiple_of(c * ROWS, ROWS), ROWS)
    far_rows = pl.ds(pl.multiple_of((1 - c) * ROWS, ROWS), ROWS)

    def remote(src, dst, ssem, rsem, to):
        return pltpu.make_async_remote_copy(
            src_ref=src, dst_ref=dst, send_sem=ssem, recv_sem=rsem, device_id=to, device_id_type=MESH
        )

    def chip_to(k):
        a, b = CHIP_STEPS[k]
        return lax.rem(yh + a, NH), lax.rem(x + b, NX)

    def chip_from(k):
        a, b = CHIP_STEPS[k]
        return lax.rem(yh + NH - a, NH) * NX + lax.rem(x + NX - b, NX)

    def seq_to(k):
        a, b = SEQ_STEPS[k]
        return lax.rem(yl + a, NY), lax.rem(z + b, NZ)

    def seq_from(k):
        a, b = SEQ_STEPS[k]
        return lax.rem(yl + NY - a, NY) * NZ + lax.rem(z + NZ - b, NZ)

    loads = [
        pltpu.make_async_copy(h, wqkv.at[:, pl.ds(i * WIDTH, WIDTH)], w_sem.at[i])
        for i, h in enumerate((wq_hbm, wk_hbm, wv_hbm))
    ]
    loads.append(pltpu.make_async_copy(wo_hbm, wo, w_sem.at[3]))
    for cp in loads:
        cp.start()

    @pl.loop(0, NZ)
    def _(i):
        for buf in (kb, vb, qb, gb):
            buf[i] = jnp.zeros((TOK, WIDTH), BF16)
        for buf in (ga2, gb2):
            buf[i] = jnp.zeros((TOK, HEAD_DIM), BF16)

    bar = pltpu.get_barrier_semaphore()
    greet = [partner]
    for k in range(len(CHIP_STEPS)):
        a, b = chip_to(k)
        greet.append(dev(yh_=a, x_=b))
    for k in range(len(SEQ_STEPS)):
        a, b = seq_to(k)
        greet.append(dev(yl_=a, z_=b))
    for g in greet:
        pl.semaphore_signal(bar, inc=1, device_id=g, device_id_type=MESH)

    pt = point_ref[...].astype(F32)
    inv = lax.rsqrt(jnp.mean(pt * pt, axis=1, keepdims=True) + EPS)
    loc[0] = pt * inv
    loc[1] = inc_ref[...].astype(F32)
    irl[...] = jnp.broadcast_to(inv, (ROWS, 128))
    pl.semaphore_wait(bar, len(greet))

    swaps = [
        remote(loc.at[0, :, far_half], sc16.at[own_rows, :], d2s.at[0], d2r.at[0], partner),
        remote(loc.at[1, :, far_half], in16.at[own_rows, :], d2s.at[1], d2r.at[1], partner),
        remote(irl, ir16.at[own_rows, :], d2s.at[2], d2r.at[2], partner),
    ]
    for cp in swaps:
        cp.start()
    sc16[own_rows, :] = loc[0, :, own_half]
    in16[own_rows, :] = loc[1, :, own_half]
    ir16[own_rows, :] = irl[...]
    gain_half = gain_ref[:, own_half]
    for cp, buf in zip(swaps, (sc16, in16, ir16)):
        cp.wait_send()
    remote(loc.at[0, :, far_half], sc16.at[far_rows, :], d2s.at[0], d2r.at[0], partner).wait_recv()
    remote(loc.at[1, :, far_half], in16.at[far_rows, :], d2s.at[1], d2r.at[1], partner).wait_recv()
    remote(irl, ir16.at[far_rows, :], d2s.at[2], d2r.at[2], partner).wait_recv()

    def gather_sends(buf, g):
        mine = buf.at[chip, :, own_half]
        out = [remote(mine, mine, ags.at[g, 7], agr.at[g, 7], partner)]
        for k in range(7):
            a, b = chip_to(k)
            out.append(remote(mine, mine, ags.at[g, k], agr.at[g, k], dev(yh_=a, x_=b)))
        return out

    def gather_start(buf, g):
        for cp in gather_sends(buf, g):
            cp.start()

    def gather_finish(buf, g):
        forwards = []
        for k in range(7):
            slot = buf.at[chip_from(k), :, own_half]
            remote(slot, slot, ags.at[g, k], agr.at[g, k], partner).wait_recv()
            cp = remote(slot, slot, fws.at[g, k], fwr.at[g, k], partner)
            cp.start()
            forwards.append(cp)
        far = buf.at[chip, :, far_half]
        remote(far, far, ags.at[g, 7], agr.at[g, 7], partner).wait_recv()
        for k in range(7):
            far = buf.at[chip_from(k), :, far_half]
            remote(far, far, fws.at[g, k], fwr.at[g, k], partner).wait_recv()
        for cp in forwards + gather_sends(buf, g):
            cp.wait_send()

    agx[chip, :, own_half] = (gain_half * sc16[...]).astype(BF16)
    gather_start(agx, 0)
    agi[chip, :, own_half] = in16[...].astype(BF16)
    gather_start(agi, 1)

    row_tok = s * TOK + lax.broadcasted_iota(jnp.int32, (TOK, 1), 0)
    row_blk = row_tok // BLK
    blk_col = lax.broadcasted_iota(jnp.int32, (TOK, NBLK), 1)
    lay = jnp.where(lay_ref[...] > 0, 1.0, 0.0).astype(BF16)
    onehot = jnp.where(blk_col == row_blk, 1.0, 0.0).astype(BF16)
    chosen_q = jnp.where(blk_col < row_blk, dot(onehot, lay), 0.0).astype(BF16)
    chosen_k = jnp.where(blk_col > row_blk, dot(onehot, lay, NT), 0.0).astype(BF16)
    for part in range(2):
        plane = yl if part == 0 else 1 - yl
        col_blk = plane * (PLANE // BLK) + lax.broadcasted_iota(jnp.int32, (NBLK, PLANE), 1) // BLK
        spread = jnp.where(lax.broadcasted_iota(jnp.int32, (NBLK, PLANE), 0) == col_blk, 1.0, 0.0)
        spread = spread.astype(BF16)
        col_tok = plane * PLANE + lax.broadcasted_iota(jnp.int32, (1, PLANE), 1)
        same = row_blk == col_tok // BLK
        ok = (dot(chosen_q, spread) > 0.5) | (same & (col_tok <= row_tok))
        bq[part] = jnp.where(ok, 0.0, MASKED)
        ok = (dot(chosen_k, spread) > 0.5) | (same & (col_tok >= row_tok))
        bk[part] = jnp.where(ok, 0.0, MASKED)

    angle = row_tok.astype(F32) * freq_ref[...]
    lower = lax.broadcasted_iota(jnp.int32, (TOK, HEAD_DIM), 1) < HEAD_DIM // 2
    cosb[...] = jnp.cos(angle)
    sine = jnp.sin(angle)
    sinb[...] = jnp.where(lower, -sine, sine)

    def turn(v, back=False):
        turned = pltpu.roll(v, HEAD_DIM // 2, 1) * sinb[...]
        return v * cosb[...] - turned if back else v * cosb[...] + turned

    for cp in loads:
        cp.wait()

    @pl.loop(0, D // 512)
    def _(j):
        rows = pl.ds(pl.multiple_of(j * 512, 512), 512)
        wqkv_t[:, rows] = jnp.transpose(wqkv[rows, :])
        wo_t[rows, :] = jnp.transpose(wo[:, rows])

    gather_finish(agx, 0)

    def depth(sgn):
        return NZ // 2 - c if sgn > 0 else NZ // 2 - 1 + c

    def wanted(stream, sgn, d, at):
        full = depth(sgn)
        near = d <= full
        if stream == OA:
            return near
        if stream == OA2:
            return near & (yl == 0)
        origin = lax.rem(at - sgn * d + NZ, NZ)
        if (stream in (K, V)) == (sgn > 0):
            some = (at >= d) if sgn > 0 else (at + d <= NZ - 1)
        else:
            some = (origin + full >= NZ) if sgn > 0 else (origin < full)
        if stream == V:
            some = some | (yl == 0)
        if stream in (G, GB):
            some = some | (yl == 1)
        return near & some

    bufs = (kb, vb, qb, gb, oa, ga2, gb2, oa2)

    def hop(stream, sgn, d, at):
        block = bufs[stream].at[lax.rem(at - sgn * (d - 1) + NZ, NZ)]
        to = dev(z_=lax.rem(z + sgn + NZ, NZ))
        i = 0 if sgn > 0 else 1
        return remote(block, block, rgs.at[stream, i, d - 1], rgr.at[stream, i, d - 1], to)

    def send_hop(stream, sgn, d):
        @pl.when(wanted(stream, sgn, d, lax.rem(z + sgn + NZ, NZ)))
        def _():
            hop(stream, sgn, d, z).start()

    across = dev(yl_=1 - yl)

    def over(stream, origin):
        dst, n = (ob2, 1) if stream == GB else (ob, 0)
        return remote(
            bufs[stream].at[origin], dst.at[origin], yfs.at[n, origin], yfr.at[n, origin], across
        )

    def send_over(stream, origin):
        @pl.when(yl == (0 if stream == V else 1))
        def _():
            over(stream, origin).start()

    def take_hop(stream, sgn, d):
        @pl.when(wanted(stream, sgn, d, z))
        def _():
            hop(stream, sgn, d, lax.rem(z - sgn + NZ, NZ)).wait_recv()
            if stream in (V, G, GB):
                send_over(stream, lax.rem(z - sgn * d + NZ, NZ))

    def ring_start(stream):
        for sgn in (1, -1):
            send_hop(stream, sgn, 1)
        if stream in (V, G, GB):
            send_over(stream, z)

    def ring_step(d, *streams):
        for stream in streams:
            for sgn in (1, -1):
                take_hop(stream, sgn, d)
                if d < NZ // 2:
                    send_hop(stream, sgn, d + 1)

    def ring_sent(*streams):
        for stream in streams:
            for d in range(1, NZ // 2 + 1):
                for sgn in (1, -1):

                    @pl.when(wanted(stream, sgn, d, lax.rem(z + sgn + NZ, NZ)))
                    def _():
                        hop(stream, sgn, d, z).wait_send()

            if stream in (V, G, GB):

                @pl.when(yl == (0 if stream == V else 1))
                def _():
                    for i in range(NZ):
                        over(stream, i).wait_send()

    def over_wait(n):
        buf = ob2 if n else ob
        for i in range(NZ):
            remote(buf.at[i], buf.at[i], yfs.at[n, i], yfr.at[n, i], across).wait_recv()

    def cross(src, dst, i):
        return remote(src.at[z], dst.at[z], yxs.at[i], yxr.at[i], across)

    def project(i):
        return dot(agx[...].reshape(TOK, D), wqkv[:, i * WIDTH : (i + 1) * WIDTH])

    def turned_into(buf, v):
        for h in range(HEADS_DEV):
            buf[z, :, h * HEAD_DIM : (h + 1) * HEAD_DIM] = turn(
                v[:, h * HEAD_DIM : (h + 1) * HEAD_DIM]
            ).astype(BF16)

    turned_into(kb, project(1))

    @pl.when(yl == 0)
    def _():
        cross(kb, oa, 0).start()

    ring_start(K)
    vb[z] = project(2).astype(BF16)
    ring_start(V)
    turned_into(qb, project(0))

    @pl.when(yl == 1)
    def _():
        cross(qb, oa, 0).start()

    ring_start(Q)
    ring_step(1, K, V)
    cross(oa, oa, 0).wait_recv()
    ring_start(OA)
    gather_finish(agi, 1)
    gb[z] = dot(agi[...].reshape(TOK, D), wo_t[...]).astype(BF16)
    ring_start(G)
    ring_step(1, Q, OA)
    ring_step(2, K, V)
    ring_step(2, Q, OA)
    ring_step(1, G)
    ring_step(3, K, V)
    ring_step(3, Q, OA)
    ring_step(2, G)
    ring_step(4, K, V)
    ring_step(4, Q, OA)
    ring_step(3, G)
    @pl.when(yl == 1)
    def _():
        over_wait(0)

    def lanes(h):
        return pl.ds(h * HEAD_DIM, HEAD_DIM)

    def rows_of(buf, h):
        return buf[:, :, lanes(h)].reshape(PLANE, HEAD_DIM)

    def as_row(col):
        return jnp.transpose(jnp.broadcast_to(col, (TOK, TOK)))[0:1, :]

    def forward(parts):
        for h in range(HEADS_DEV):
            query = qb[z, :, lanes(h)]
            top = None
            for i, (buf, _) in enumerate(parts):
                sc = dot(query, rows_of(buf, h), NT) * scale + bq[i]
                pq[h, i] = sc
                m = jnp.max(sc, axis=1, keepdims=True)
                top = m if top is None else jnp.maximum(top, m)
            total = None
            for i in range(len(parts)):
                e = jnp.exp(pq[h, i] - top)
                pq[h, i] = e
                l = jnp.sum(e, axis=1, keepdims=True)
                total = l if total is None else total + l
            inv_total = 1.0 / total
            out = None
            for i, (_, buf) in enumerate(parts):
                p = pq[h, i] * inv_total
                pq[h, i] = p
                o = dot(p.astype(BF16), rows_of(buf, h))
                out = o if out is None else out + o
            out = out.astype(BF16)
            att[:, lanes(h)] = out
            grad = gb[z, :, lanes(h)]
            st[0, s, pl.ds(h, 1), :] = as_row(top + jnp.log(total))
            st[0, s, pl.ds(2 + h, 1), :] = as_row(
                jnp.sum(grad.astype(F32) * out.astype(F32), axis=1, keepdims=True)
            )

    @pl.when(yl == 0)
    def _():
        forward(((kb, vb),))

    @pl.when(yl == 1)
    def _():
        forward(((kb, vb), (oa, ob)))

    def stats_sends(it):
        out = []
        for k in range(len(SEQ_STEPS)):
            a, b = seq_to(k)
            mine = st.at[it, s]
            out.append(remote(mine, mine, sts.at[it, k], str_.at[it, k], dev(yl_=a, z_=b)))
        return out

    def stats_wait(it):
        for k in range(len(SEQ_STEPS)):
            slot = st.at[it, seq_from(k)]
            remote(slot, slot, sts.at[it, k], str_.at[it, k], partner).wait_recv()
        for cp in stats_sends(it):
            cp.wait_send()

    def own_grad(it, h):
        return gb[z, :, lanes(h)] if it == 0 else (ga2, gb2)[h][z]

    def query_side(it, parts):
        for h in range(HEADS_DEV):
            grad = own_grad(it, h)
            delta = jnp.sum(
                grad.astype(F32) * att[:, lanes(h)].astype(F32), axis=1, keepdims=True
            )
            out = None
            for i, (keys, values) in enumerate(parts):
                gp = dot(grad, rows_of(values, h), NT)
                gsc = (pq[h, i] * (gp - delta)).astype(BF16)
                o = dot(gsc, rows_of(keys, h))
                out = o if out is None else out + o
            dqkv[:, lanes(h)] = turn(out * scale, True).astype(BF16)

    def key_side(it, parts, planes):
        for h in range(HEADS_DEV):
            key = kb[z, :, lanes(h)]
            value = vb[z, :, lanes(h)]
            gk, gv = None, None
            for i, (queries, grads, late) in enumerate(parts):
                row = lambda n, r: jnp.concatenate(
                    [st[n, planes[i] * NZ + j, pl.ds(r, 1), :] for j in range(NZ)], axis=1
                )
                query = rows_of(queries, h)
                if it == 0:
                    p = jnp.exp(dot(key, query, NT) * scale + bk[i] - row(0, h))
                    pk[h, i] = p
                    grad = rows_of(grads, h)
                else:
                    p = pk[h, i]
                    grad = late[h][...].reshape(PLANE, HEAD_DIM)
                v = dot(p.astype(BF16), grad)
                gv = v if gv is None else gv + v
                gp = dot(value, grad, NT)
                gsc = (p * (gp - row(it, 2 + h))).astype(BF16)
                k = dot(gsc, query)
                gk = k if gk is None else gk + k
            dqkv[:, lanes(HEADS_DEV + h)] = turn(gk * scale, True).astype(BF16)
            dqkv[:, lanes(2 * HEADS_DEV + h)] = gv.astype(BF16)

    def backward(it):
        @pl.when(yl == 0)
        def _():
            query_side(it, ((kb, vb),))

        @pl.when(yl == 1)
        def _():
            query_side(it, ((kb, vb), (oa, ob)))

        stats_wait(it)

        @pl.when(yl == 0)
        def _():
            over_wait(it)

        @pl.when(yl == 0)
        def _():
            key_side(it, ((qb, gb, (ga2, gb2)), (oa, ob, (oa2, ob2))), (yl, 1 - yl))

        @pl.when(yl == 1)
        def _():
            key_side(it, ((qb, gb, (ga2, gb2)),), (yl,))

        wide = HALF // CHUNKS
        gives = []
        for j in range(CHUNKS):
            cols = pl.ds(pl.multiple_of((1 - c) * HALF + j * wide, wide), wide)
            tot[it, j] = dot(dqkv[...], wqkv_t[:, cols]).astype(BF16).reshape(CHIPS, CROWS, wide)
            cp = remote(tot.at[it, j], drv.at[it, j], gvs.at[it, j], gvr.at[it, j], partner)
            cp.start()
            gives.append(cp)
        sends = []
        for j in range(CHUNKS):
            cols = pl.ds(pl.multiple_of(c * HALF + j * wide, wide), wide)
            mine = dot(dqkv[...], wqkv_t[:, cols]).reshape(CHIPS, CROWS, wide)
            gives[j].wait_recv()
            pair[...] = mine + drv[it, j].astype(F32)
            for k in range(7):
                a, b = chip_to(k)
                rsrc[it, j, k] = pair[a * NX + b].astype(BF16)
                cp = remote(
                    rsrc.at[it, j, k], rrv.at[it, j, k], rss.at[it, j, k], rsr.at[it, j, k],
                    dev(yh_=a, x_=b),
                )
                cp.start()
                sends.append(cp)
            here = pl.ds(j * wide, wide)
            gn[:, here] = pair[chip]
            term = jnp.sum(
                (pair[...] * agx[:, :, cols].astype(F32)).reshape(TOK, wide), axis=0, keepdims=True
            )
            gacc[:, here] = term if it == 0 else gacc[:, here] + term
        if it == ITERS - 1:
            gt[chip] = gacc[...]
            sends.extend(gain_chip_sends())
            for cp in gain_chip_sends():
                cp.start()
            for k in range(7):
                slot = gt.at[chip_from(k)]
                remote(slot, slot, gts.at[k], gtr.at[k], partner).wait_recv()
            acc = gt[0]
            for i in range(1, CHIPS):
                acc = acc + gt[i]
            gs[s] = acc
            sends.extend(gain_seq_sends())
            for cp in gain_seq_sends():
                cp.start()
        for j in range(CHUNKS):
            here = pl.ds(j * wide, wide)
            for k in range(7):
                sends[7 * j + k].wait_recv()
                gn[:, here] += rrv[it, j, k].astype(F32)

        grad_normed = gn[...]
        scaled = sc16[...]
        weighted = gain_half * grad_normed
        inl[it] = jnp.broadcast_to(
            jnp.sum(weighted * scaled, axis=1, keepdims=True), (CROWS, 128)
        )
        share = remote(inl.at[it], inr.at[it], d2s.at[5 + it], d2r.at[5 + it], partner)
        share.start()
        share.wait_recv()
        inner = (inl[it] + inr[it])[:, 0:1]
        cot = ir16[:, 0:1] * (weighted - scaled * (inner / D))
        adj16[...] = (in16[...] if it == 0 else adj16[...]) + cot
        if it == 0:
            agc[chip, :, own_half] = cot.astype(BF16)
            gather_start(agc, 2)
        for cp in gives + [share] + sends:
            cp.wait_send()

    def gain_chip_sends():
        out = []
        for k in range(7):
            a, b = chip_to(k)
            out.append(
                remote(gt.at[chip], gt.at[chip], gts.at[k], gtr.at[k], dev(yh_=a, x_=b))
            )
        return out

    def gain_seq_sends():
        out = []
        for k in range(len(SEQ_STEPS)):
            a, b = seq_to(k)
            out.append(remote(gs.at[s], gs.at[s], gss.at[k], gsr.at[k], dev(yl_=a, z_=b)))
        return out

    for cp in stats_sends(0):
        cp.start()
    ring_step(4, G)
    backward(0)

    ring_sent(K, V, Q, G, OA)

    @pl.when(yl == 0)
    def _():
        cross(kb, oa, 0).wait_send()

    @pl.when(yl == 1)
    def _():
        cross(qb, oa, 0).wait_send()

    gather_finish(agc, 2)
    grad2 = dot(agc[...].reshape(TOK, D), wo_t[...]).astype(BF16)
    ga2[z] = grad2[:, :HEAD_DIM]
    gb2[z] = grad2[:, HEAD_DIM:]

    @pl.when(yl == 1)
    def _():
        cross(ga2, oa2, 1).start()

    ring_start(GB)
    ring_start(GA)
    for h in range(HEADS_DEV):
        st[1, s, pl.ds(2 + h, 1), :] = as_row(
            jnp.sum(
                own_grad(1, h).astype(F32) * att[:, lanes(h)].astype(F32), axis=1, keepdims=True
            )
        )
    for cp in stats_sends(1):
        cp.start()
    ring_step(1, GB)

    @pl.when(yl == 0)
    def _():
        cross(oa2, oa2, 1).wait_recv()

    ring_start(OA2)
    ring_step(1, GA)
    ring_step(2, GB)
    ring_step(1, OA2)
    ring_step(2, GA)
    ring_step(3, GB)
    ring_step(2, OA2)
    ring_step(3, GA)
    ring_step(4, GB)
    ring_step(3, OA2)
    ring_step(4, GA)
    ring_step(4, OA2)
    backward(1)

    back = remote(adj16.at[far_rows, :], adjr, d2s.at[7], d2r.at[7], partner)
    back.start()
    adj_ref[:, own_half] = adj16[own_rows, :]
    for k in range(len(SEQ_STEPS)):
        slot = gs.at[seq_from(k)]
        remote(slot, slot, gss.at[k], gsr.at[k], partner).wait_recv()
    acc = gs[0]
    for i in range(1, NY * NZ):
        acc = acc + gs[i]
    gh[0] = acc / gain_half * (NY * NZ * TOK) ** (-0.5)
    last = remote(gh.at[0], gh.at[1], d2s.at[8], d2r.at[8], partner)
    last.start()
    back.wait_recv()
    adj_ref[:, far_half] = adjr[...]
    gg_ref[:, own_half] = gh[0]
    last.wait_recv()
    gg_ref[:, far_half] = gh[1]
    ring_sent(GA, GB, OA2)

    @pl.when(yl == 1)
    def _():
        cross(ga2, oa2, 1).wait_send()

    for cp in [back, last]:
        cp.wait_send()


def scratch():
    v = pltpu.VMEM
    dma = pltpu.SemaphoreType.DMA
    wide = HALF // CHUNKS
    block = (NZ, TOK, WIDTH)
    half_block = (NZ, TOK, HEAD_DIM)
    return [
        v((D, 3 * WIDTH), BF16), v((WIDTH, D), BF16), v((3 * WIDTH, D), BF16), v((D, WIDTH), BF16),
        v((TOK, HEAD_DIM), F32), v((TOK, HEAD_DIM), F32),
        v((2, ROWS, D), F32), v((CROWS, HALF), F32), v((CROWS, HALF), F32), v((CROWS, 128), F32),
        v((ROWS, 128), F32),
        v((CHIPS, CROWS, D), BF16), v((CHIPS, CROWS, D), BF16), v((CHIPS, CROWS, D), BF16),
        v(block, BF16), v(block, BF16), v(block, BF16), v(block, BF16), v(block, BF16),
        v(block, BF16),
        v(half_block, BF16), v(half_block, BF16), v(half_block, BF16), v(half_block, BF16),
        v((ITERS, NY * NZ, 8, TOK), F32),
        v((2, TOK, PLANE), F32), v((2, TOK, PLANE), F32),
        v((HEADS_DEV, 2, TOK, PLANE), F32), v((HEADS_DEV, 2, TOK, PLANE), F32),
        v((TOK, WIDTH), BF16), v((TOK, 3 * WIDTH), BF16),
        v((ITERS, CHUNKS, CHIPS, CROWS, wide), BF16), v((ITERS, CHUNKS, CHIPS, CROWS, wide), BF16),
        v((ITERS, CHUNKS, 7, CROWS, wide), BF16), v((ITERS, CHUNKS, 7, CROWS, wide), BF16),
        v((CHIPS, CROWS, wide), F32), v((CROWS, HALF), F32),
        v((ITERS, CROWS, 128), F32), v((ITERS, CROWS, 128), F32),
        v((CROWS, HALF), F32), v((ROWS, HALF), F32), v((1, HALF), F32),
        v((CHIPS, 1, HALF), F32), v((NY * NZ, 1, HALF), F32), v((2, 1, HALF), F32),
        dma((4,)), dma((3, 8)), dma((3, 8)), dma((3, 7)), dma((3, 7)), dma((9,)), dma((9,)),
        dma((8, 2, 4)), dma((8, 2, 4)), dma((2,)), dma((2,)), dma((2, NZ)), dma((2, NZ)),
        dma((ITERS, 15)), dma((ITERS, 15)), dma((ITERS, CHUNKS)), dma((ITERS, CHUNKS)),
        dma((ITERS, CHUNKS, 7)), dma((ITERS, CHUNKS, 7)),
        dma((7,)), dma((7,)), dma((15,)), dma((15,)),
    ]


def body(
    fixed_point, incoming, norm_gain, query_weight, key_weight, value_weight, out_weight, layout
):
    pair = lax.rem(jnp.arange(HEAD_DIM, dtype=jnp.int32), HEAD_DIM // 2).astype(F32)
    freq = THETA ** (-2.0 * pair / HEAD_DIM)
    vmem = pl.BlockSpec(memory_space=pltpu.VMEM)
    hbm = pl.BlockSpec(memory_space=pl.ANY)
    adjoint, gain = pl.pallas_call(
        kernel,
        out_shape=(
            jax.ShapeDtypeStruct((ROWS, D), F32),
            jax.ShapeDtypeStruct((1, D), F32),
        ),
        in_specs=[vmem] * 5 + [hbm] * 4,
        out_specs=(vmem, vmem),
        scratch_shapes=scratch(),
        compiler_params=pltpu.CompilerParams(
            collective_id=0, has_side_effects=True, vmem_limit_bytes=62 * 1024 * 1024
        ),
        name="deq_backward",
    )(
        fixed_point, incoming, norm_gain[None, :], freq[None, :], layout,
        query_weight, key_weight, value_weight, out_weight,
    )
    return adjoint, gain[0]


def solution(mesh):
    split = Mesh(mesh.devices.reshape(NY, NZ, NH, NX, NC), AXES)
    in_specs = (
        P(SEQ_TENSOR, None),
        P(SEQ_TENSOR, None),
        P(),
        P(None, TENSOR),
        P(None, TENSOR),
        P(None, TENSOR),
        P(TENSOR, None),
        P(),
    )
    out_specs = (P(SEQ_TENSOR, None), P())
    return jax.shard_map(body, mesh=split, in_specs=in_specs, out_specs=out_specs, check_vma=False)
```

time: 147 us -> 127 us (0.86)
  Pallas kernels: 140 us -> 122 us
  other arithmetic: 2.4 us -> 0.52 us
    pallas_call x1, Pallas kernels: 140 us -> 122 us  [body(): pl.pallas_call(kernel, out_shape=(jax.ShapeDtypeStruct((ROWS, D), F32), j...]
where the time goes in v2:
time: 127 us; the launch traced here: 126 us
  Pallas kernels  122 us (96%)
  local copies, waits for them, and re-layouts  2.89 us (2%)
    pallas_call x1, Pallas kernels, body(): pl.pallas_call(kernel, out_shape=(jax.ShapeDtypeStruct((ROWS, D), F32), j...  122 us
    unnamed x2, local copies, waits for them, and re-layouts  2.89 us

profile of v2, /device:TPU:1, one launch (start us, length us, event | category | flops | bytes accessed | tf_op | source)
XLA Modules:
  0.0 126.4 jit_solution(6744064382589878960)
XLA Ops:
  0.6 0.5 multiply_power_fusion.freq_ref
  1.2 122.3 %deq_backward.1 = (f32[8,4096]{1,0:T(8,128)}, f32[1,4096]{1,0:T(1,128)}) custom-call(bf16[8,4096]{1,0:T(8,128)(2,1)} %point_ref.1, bf16[8,4096]{1,0:T(8,128)(2,1)} %inc_ref.1, f32[1,4096]{1,0:T(1,128)} %bitcast.2, f32[1,128]{1,0:T(1,128)} %multiply_power_fusion.freq_ref, s32[32,32]{1,0:T(8,128)} %lay_ref.1, bf16[4096,256]{1,0:T(8,128)(2,1)} %wq_hbm.1, ...), custom_call_target="tpu_custom_call" | custom-call | tf_op jit(solution)/shard_map/deq_backward/pallas_call | solution.py:688
  123.5 1.6 %copy.12 = f32[8,4096]{1,0:T(8,128)} copy(f32[8,4096]{1,0:T(8,128)} %get-tuple-element.8) | data formatting | bytes 262144
  125.1 1.3 %copy.13 = f32[4096]{0:T(1024)} copy(f32[4096]{0:T(1024)} %bitcast.3) | data formatting | bytes 32768

commit v3 on v2

--- a/solution.py
+++ b/solution.py
@@ -2,6 +2,7 @@
 
 import jax
 import jax.numpy as jnp
+import numpy as np
 from jax import lax
 from jax.experimental import pallas as pl
 from jax.experimental.pallas import tpu as pltpu
@@ -49,12 +50,13 @@
 
 
 def kernel(
-    point_ref, inc_ref, gain_ref, freq_ref, lay_ref, wq_hbm, wk_hbm, wv_hbm, wo_hbm,
+    point_hbm, inc_hbm, gain_hbm, freq_hbm, lay_hbm, wq_hbm, wk_hbm, wv_hbm, wo_hbm,
     adj_ref, gg_ref,
+    point_ref, inc_ref, gain_ref, freq_ref, lay_ref,
     wqkv, wo, wqkv_t, wo_t, cosb, sinb, loc, sc16, in16, ir16, irl, agx, agi, agc,
     kb, vb, qb, gb, oa, ob, ga2, gb2, oa2, ob2, st, bq, bk, pq, pk, att, dqkv,
     tot, drv, rsrc, rrv, pair, gn, inl, inr, adj16, adjr, gacc, gt, gs, gh,
-    w_sem, ags, agr, fws, fwr, d2s, d2r, rgs, rgr, yxs, yxr, yfs, yfr, sts, str_,
+    in_sem, w_sem, ags, agr, fws, fwr, d2s, d2r, rgs, rgr, yxs, yxr, yfs, yfr, sts, str_,
     gvs, gvr, rss, rsr, gts, gtr, gss, gsr,
 ):
     yl, z, yh, x, c = (lax.axis_index(a) for a in AXES)
@@ -67,6 +69,7 @@
         return (pick(yl, yl_), pick(z, z_), pick(yh, yh_), pick(x, x_), pick(c, c_))
 
     partner = dev(c_=1 - c)
+    sent = []
     own_half = pl.ds(pl.multiple_of(c * HALF, HALF), HALF)
     far_half = pl.ds(pl.multiple_of((1 - c) * HALF, HALF), HALF)
     own_rows = pl.ds(pl.multiple_of(c * ROWS, ROWS), ROWS)
@@ -93,6 +96,15 @@
         a, b = SEQ_STEPS[k]
         return lax.rem(yl + NY - a, NY) * NZ + lax.rem(z + NZ - b, NZ)
 
+    small = [
+        pltpu.make_async_copy(h, v, in_sem.at[i])
+        for i, (h, v) in enumerate(
+            ((point_hbm, point_ref), (inc_hbm, inc_ref), (gain_hbm, gain_ref),
+             (freq_hbm, freq_ref), (lay_hbm, lay_ref))
+        )
+    ]
+    for cp in small:
+        cp.start()
     loads = [
         pltpu.make_async_copy(h, wqkv.at[:, pl.ds(i * WIDTH, WIDTH)], w_sem.at[i])
         for i, h in enumerate((wq_hbm, wk_hbm, wv_hbm))
@@ -119,6 +131,8 @@
     for g in greet:
         pl.semaphore_signal(bar, inc=1, device_id=g, device_id_type=MESH)
 
+    for cp in small:
+        cp.wait()
     pt = point_ref[...].astype(F32)
     inv = lax.rsqrt(jnp.mean(pt * pt, axis=1, keepdims=True) + EPS)
     loc[0] = pt * inv
@@ -155,20 +169,24 @@
         for cp in gather_sends(buf, g):
             cp.start()
 
-    def gather_finish(buf, g):
-        forwards = []
+    def gather_pass(buf, g):
         for k in range(7):
             slot = buf.at[chip_from(k), :, own_half]
             remote(slot, slot, ags.at[g, k], agr.at[g, k], partner).wait_recv()
-            cp = remote(slot, slot, fws.at[g, k], fwr.at[g, k], partner)
-            cp.start()
-            forwards.append(cp)
+            remote(slot, slot, fws.at[g, k], fwr.at[g, k], partner).start()
+
+    def gather_finish(buf, g):
         far = buf.at[chip, :, far_half]
         remote(far, far, ags.at[g, 7], agr.at[g, 7], partner).wait_recv()
         for k in range(7):
             far = buf.at[chip_from(k), :, far_half]
             remote(far, far, fws.at[g, k], fwr.at[g, k], partner).wait_recv()
-        for cp in forwards + gather_sends(buf, g):
+
+    def gather_sent(buf, g):
+        for k in range(7):
+            slot = buf.at[chip_from(k), :, own_half]
+            remote(slot, slot, fws.at[g, k], fwr.at[g, k], partner).wait_send()
+        for cp in gather_sends(buf, g):
             cp.wait_send()
 
     agx[chip, :, own_half] = (gain_half * sc16[...]).astype(BF16)
@@ -214,6 +232,7 @@
         wqkv_t[:, rows] = jnp.transpose(wqkv[rows, :])
         wo_t[rows, :] = jnp.transpose(wo[:, rows])
 
+    gather_pass(agx, 0)
     gather_finish(agx, 0)
 
     def depth(sgn):
@@ -224,8 +243,6 @@
         near = d <= full
         if stream == OA:
             return near
-        if stream == OA2:
-            return near & (yl == 0)
         origin = lax.rem(at - sgn * d + NZ, NZ)
         if (stream in (K, V)) == (sgn > 0):
             some = (at >= d) if sgn > 0 else (at + d <= NZ - 1)
@@ -233,7 +250,7 @@
             some = (origin + full >= NZ) if sgn > 0 else (origin < full)
         if stream == V:
             some = some | (yl == 0)
-        if stream in (G, GB):
+        if stream == G:
             some = some | (yl == 1)
         return near & some
 
@@ -304,6 +321,79 @@
         for i in range(NZ):
             remote(buf.at[i], buf.at[i], yfs.at[n, i], yfr.at[n, i], across).wait_recv()
 
+    def wanted2(stream, sgn, d, at):
+        full = depth(sgn)
+        near = d <= full
+        if stream == OA2:
+            return near & (yl == 0)
+        origin = lax.rem(at - sgn * d + NZ, NZ)
+        if sgn < 0:
+            some = origin >= d
+        else:
+            some = origin + (full if d == 2 else d) >= NZ
+        if stream == GB:
+            some = some | (yl == 1)
+        return near & some
+
+    def far_hop(stream, sgn, d, at):
+        base, step = ((0, 1), (0, 2), (2, 1), (2, 2))[d - 1]
+        origin = lax.rem(at - sgn * base + NZ, NZ)
+        block = bufs[stream].at[origin]
+        z_to = lax.rem(z + sgn * step + NZ, NZ)
+        i = 0 if sgn > 0 else 1
+        sems = rgs.at[stream, i, d - 1], rgr.at[stream, i, d - 1]
+        if stream == OA2 and d == 2:
+            return remote(ga2.at[origin], block, *sems, dev(yl_=1 - yl, z_=z_to))
+        return remote(block, block, *sems, dev(z_=z_to))
+
+    def far_cond(stream, sgn, d):
+        step = (1, 2, 1, 2)[d - 1]
+        if stream == OA2 and d == 2:
+            return yl == 1
+        return wanted2(stream, sgn, d, lax.rem(z + sgn * step + NZ, NZ))
+
+    def far_send(stream, *ds):
+        for d in ds:
+            for sgn in (1, -1):
+
+                @pl.when(far_cond(stream, sgn, d))
+                def _():
+                    far_hop(stream, sgn, d, z).start()
+
+    def far_take(stream, *ds):
+        for d in ds:
+            for sgn in (1, -1):
+
+                @pl.when(wanted2(stream, sgn, d, z))
+                def _():
+                    step = (1, 2, 1, 2)[d - 1]
+                    far_hop(stream, sgn, d, lax.rem(z - sgn * step + NZ, NZ)).wait_recv()
+                    if stream == GB:
+                        send_over(stream, lax.rem(z - sgn * d + NZ, NZ))
+
+                if d == 2:
+                    for e in (4, 3):
+
+                        @pl.when(far_cond(stream, sgn, e))
+                        def _():
+                            far_hop(stream, sgn, e, z).start()
+
+    def far_sent(*streams):
+        for stream in streams:
+            for d in range(1, NZ // 2 + 1):
+                for sgn in (1, -1):
+
+                    @pl.when(far_cond(stream, sgn, d))
+                    def _():
+                        far_hop(stream, sgn, d, z).wait_send()
+
+            if stream == GB:
+
+                @pl.when(yl == 1)
+                def _():
+                    for i in range(NZ):
+                        over(stream, i).wait_send()
+
     def cross(src, dst, i):
         return remote(src.at[z], dst.at[z], yxs.at[i], yxr.at[i], across)
 
@@ -331,23 +421,25 @@
     def _():
         cross(qb, oa, 0).start()
 
-    ring_start(Q)
-    ring_step(1, K, V)
+    ring_step(1, K)
+    gather_pass(agi, 1)
+    ring_step(1, V)
     cross(oa, oa, 0).wait_recv()
     ring_start(OA)
+    ring_start(Q)
     gather_finish(agi, 1)
     gb[z] = dot(agi[...].reshape(TOK, D), wo_t[...]).astype(BF16)
     ring_start(G)
-    ring_step(1, Q, OA)
+    ring_step(1, OA)
     ring_step(2, K, V)
-    ring_step(2, Q, OA)
-    ring_step(1, G)
+    ring_step(2, OA)
+    ring_step(1, Q, G)
     ring_step(3, K, V)
-    ring_step(3, Q, OA)
-    ring_step(2, G)
+    ring_step(3, OA)
+    ring_step(2, Q, G)
     ring_step(4, K, V)
-    ring_step(4, Q, OA)
-    ring_step(3, G)
+    ring_step(4, OA)
+    ring_step(3, Q, G)
     @pl.when(yl == 1)
     def _():
         over_wait(0)
@@ -411,8 +503,6 @@
         for k in range(len(SEQ_STEPS)):
             slot = st.at[it, seq_from(k)]
             remote(slot, slot, sts.at[it, k], str_.at[it, k], partner).wait_recv()
-        for cp in stats_sends(it):
-            cp.wait_send()
 
     def own_grad(it, h):
         return gb[z, :, lanes(h)] if it == 0 else (ga2, gb2)[h][z]
@@ -457,7 +547,7 @@
             dqkv[:, lanes(HEADS_DEV + h)] = turn(gk * scale, True).astype(BF16)
             dqkv[:, lanes(2 * HEADS_DEV + h)] = gv.astype(BF16)
 
-    def backward(it):
+    def own_queries(it):
         @pl.when(yl == 0)
         def _():
             query_side(it, ((kb, vb),))
@@ -466,6 +556,7 @@
         def _():
             query_side(it, ((kb, vb), (oa, ob)))
 
+    def backward(it):
         stats_wait(it)
 
         @pl.when(yl == 0)
@@ -489,41 +580,51 @@
             cp.start()
             gives.append(cp)
         sends = []
+        last_term = it == ITERS - 1
         for j in range(CHUNKS):
             cols = pl.ds(pl.multiple_of(c * HALF + j * wide, wide), wide)
-            mine = dot(dqkv[...], wqkv_t[:, cols]).reshape(CHIPS, CROWS, wide)
-            gives[j].wait_recv()
-            pair[...] = mine + drv[it, j].astype(F32)
+            pair[j] = dot(dqkv[...], wqkv_t[:, cols]).reshape(CHIPS, CROWS, wide)
+
+        def scatter(j):
             for k in range(7):
                 a, b = chip_to(k)
-                rsrc[it, j, k] = pair[a * NX + b].astype(BF16)
+                rsrc[it, j, k] = pair[j, a * NX + b].astype(BF16)
                 cp = remote(
                     rsrc.at[it, j, k], rrv.at[it, j, k], rss.at[it, j, k], rsr.at[it, j, k],
                     dev(yh_=a, x_=b),
                 )
                 cp.start()
                 sends.append(cp)
+
+        for j in range(CHUNKS):
+            gives[j].wait_recv()
+            pair[j] += drv[it, j].astype(F32)
+            if not last_term:
+                scatter(j)
+        for j in range(CHUNKS):
+            cols = pl.ds(pl.multiple_of(c * HALF + j * wide, wide), wide)
             here = pl.ds(j * wide, wide)
-            gn[:, here] = pair[chip]
             term = jnp.sum(
-                (pair[...] * agx[:, :, cols].astype(F32)).reshape(TOK, wide), axis=0, keepdims=True
+                (pair[j] * agx[:, :, cols].astype(F32)).reshape(TOK, wide), axis=0, keepdims=True
             )
             gacc[:, here] = term if it == 0 else gacc[:, here] + term
-        if it == ITERS - 1:
-            gt[chip] = gacc[...]
-            sends.extend(gain_chip_sends())
+            gn[:, here] = pair[j, chip]
+        if last_term:
+            gs[s] = gacc[...]
+            for cp in gain_seq_sends():
+                cp.start()
+            for j in range(CHUNKS):
+                scatter(j)
+            for k in range(len(SEQ_STEPS)):
+                slot = gs.at[seq_from(k)]
+                remote(slot, slot, gss.at[k], gsr.at[k], partner).wait_recv()
+            acc = gs[0]
+            for i in range(1, NY * NZ):
+                acc = acc + gs[i]
+            gt[chip] = acc
             for cp in gain_chip_sends():
                 cp.start()
-            for k in range(7):
-                slot = gt.at[chip_from(k)]
-                remote(slot, slot, gts.at[k], gtr.at[k], partner).wait_recv()
-            acc = gt[0]
-            for i in range(1, CHIPS):
-                acc = acc + gt[i]
-            gs[s] = acc
-            sends.extend(gain_seq_sends())
-            for cp in gain_seq_sends():
-                cp.start()
+            sent.extend(gain_seq_sends() + gain_chip_sends())
         for j in range(CHUNKS):
             here = pl.ds(j * wide, wide)
             for k in range(7):
@@ -545,8 +646,7 @@
         if it == 0:
             agc[chip, :, own_half] = cot.astype(BF16)
             gather_start(agc, 2)
-        for cp in gives + [share] + sends:
-            cp.wait_send()
+        sent.extend(gives + [share] + sends)
 
     def gain_chip_sends():
         out = []
@@ -566,30 +666,27 @@
 
     for cp in stats_sends(0):
         cp.start()
-    ring_step(4, G)
+    ring_step(4, Q, G)
+    own_queries(0)
     backward(0)
 
-    ring_sent(K, V, Q, G, OA)
-
-    @pl.when(yl == 0)
-    def _():
-        cross(kb, oa, 0).wait_send()
-
-    @pl.when(yl == 1)
-    def _():
-        cross(qb, oa, 0).wait_send()
-
+    gather_pass(agc, 2)
     gather_finish(agc, 2)
     grad2 = dot(agc[...].reshape(TOK, D), wo_t[...]).astype(BF16)
     ga2[z] = grad2[:, :HEAD_DIM]
     gb2[z] = grad2[:, HEAD_DIM:]
 
+    far_send(OA2, 2)
+    far_send(GB, 2)
+
     @pl.when(yl == 1)
     def _():
         cross(ga2, oa2, 1).start()
 
-    ring_start(GB)
-    ring_start(GA)
+    far_send(GA, 2)
+    far_send(GB, 1)
+    send_over(GB, z)
+    far_send(GA, 1)
     for h in range(HEADS_DEV):
         st[1, s, pl.ds(2 + h, 1), :] = as_row(
             jnp.sum(
@@ -598,35 +695,32 @@
         )
     for cp in stats_sends(1):
         cp.start()
-    ring_step(1, GB)
+    own_queries(1)
+    far_take(GB, 2)
+    far_take(OA2, 2)
+    far_take(GA, 2)
 
     @pl.when(yl == 0)
     def _():
         cross(oa2, oa2, 1).wait_recv()
 
-    ring_start(OA2)
-    ring_step(1, GA)
-    ring_step(2, GB)
-    ring_step(1, OA2)
-    ring_step(2, GA)
-    ring_step(3, GB)
-    ring_step(2, OA2)
-    ring_step(3, GA)
-    ring_step(4, GB)
-    ring_step(3, OA2)
-    ring_step(4, GA)
-    ring_step(4, OA2)
+    far_send(OA2, 1)
+    far_take(GB, 1)
+    far_take(GA, 1)
+    far_take(GB, 3, 4)
+    far_take(OA2, 1, 3, 4)
+    far_take(GA, 3, 4)
     backward(1)
 
     back = remote(adj16.at[far_rows, :], adjr, d2s.at[7], d2r.at[7], partner)
     back.start()
     adj_ref[:, own_half] = adj16[own_rows, :]
-    for k in range(len(SEQ_STEPS)):
-        slot = gs.at[seq_from(k)]
-        remote(slot, slot, gss.at[k], gsr.at[k], partner).wait_recv()
-    acc = gs[0]
-    for i in range(1, NY * NZ):
-        acc = acc + gs[i]
+    for k in range(7):
+        slot = gt.at[chip_from(k)]
+        remote(slot, slot, gts.at[k], gtr.at[k], partner).wait_recv()
+    acc = gt[0]
+    for i in range(1, CHIPS):
+        acc = acc + gt[i]
     gh[0] = acc / gain_half * (NY * NZ * TOK) ** (-0.5)
     last = remote(gh.at[0], gh.at[1], d2s.at[8], d2r.at[8], partner)
     last.start()
@@ -635,13 +729,25 @@
     gg_ref[:, own_half] = gh[0]
     last.wait_recv()
     gg_ref[:, far_half] = gh[1]
-    ring_sent(GA, GB, OA2)
+    ring_sent(K, V, Q, G, OA)
+    far_sent(GA, GB, OA2)
+    gather_sent(agx, 0)
+    gather_sent(agi, 1)
+    gather_sent(agc, 2)
+
+    @pl.when(yl == 0)
+    def _():
+        cross(kb, oa, 0).wait_send()
 
     @pl.when(yl == 1)
     def _():
+        cross(qb, oa, 0).wait_send()
+
+    @pl.when(yl == 1)
+    def _():
         cross(ga2, oa2, 1).wait_send()
 
-    for cp in [back, last]:
+    for cp in sent + stats_sends(0) + stats_sends(1) + [back, last]:
         cp.wait_send()
 
 
@@ -652,6 +758,8 @@
     block = (NZ, TOK, WIDTH)
     half_block = (NZ, TOK, HEAD_DIM)
     return [
+        v((ROWS, D), BF16), v((ROWS, D), BF16), v((1, D), F32), v((1, HEAD_DIM), F32),
+        v((NBLK, NBLK), jnp.int32),
         v((D, 3 * WIDTH), BF16), v((WIDTH, D), BF16), v((3 * WIDTH, D), BF16), v((D, WIDTH), BF16),
         v((TOK, HEAD_DIM), F32), v((TOK, HEAD_DIM), F32),
         v((2, ROWS, D), F32), v((CROWS, HALF), F32), v((CROWS, HALF), F32), v((CROWS, 128), F32),
@@ -666,11 +774,11 @@
         v((TOK, WIDTH), BF16), v((TOK, 3 * WIDTH), BF16),
         v((ITERS, CHUNKS, CHIPS, CROWS, wide), BF16), v((ITERS, CHUNKS, CHIPS, CROWS, wide), BF16),
         v((ITERS, CHUNKS, 7, CROWS, wide), BF16), v((ITERS, CHUNKS, 7, CROWS, wide), BF16),
-        v((CHIPS, CROWS, wide), F32), v((CROWS, HALF), F32),
+        v((CHUNKS, CHIPS, CROWS, wide), F32), v((CROWS, HALF), F32),
         v((ITERS, CROWS, 128), F32), v((ITERS, CROWS, 128), F32),
         v((CROWS, HALF), F32), v((ROWS, HALF), F32), v((1, HALF), F32),
         v((CHIPS, 1, HALF), F32), v((NY * NZ, 1, HALF), F32), v((2, 1, HALF), F32),
-        dma((4,)), dma((3, 8)), dma((3, 8)), dma((3, 7)), dma((3, 7)), dma((9,)), dma((9,)),
+        dma((5,)), dma((4,)), dma((3, 8)), dma((3, 8)), dma((3, 7)), dma((3, 7)), dma((9,)), dma((9,)),
         dma((8, 2, 4)), dma((8, 2, 4)), dma((2,)), dma((2,)), dma((2, NZ)), dma((2, NZ)),
         dma((ITERS, 15)), dma((ITERS, 15)), dma((ITERS, CHUNKS)), dma((ITERS, CHUNKS)),
         dma((ITERS, CHUNKS, 7)), dma((ITERS, CHUNKS, 7)),
@@ -681,8 +789,8 @@
 def body(
     fixed_point, incoming, norm_gain, query_weight, key_weight, value_weight, out_weight, layout
 ):
-    pair = lax.rem(jnp.arange(HEAD_DIM, dtype=jnp.int32), HEAD_DIM // 2).astype(F32)
-    freq = THETA ** (-2.0 * pair / HEAD_DIM)
+    pair = np.arange(HEAD_DIM) % (HEAD_DIM // 2)
+    freq = jnp.asarray(THETA ** (-2.0 * pair / HEAD_DIM), F32)
     vmem = pl.BlockSpec(memory_space=pltpu.VMEM)
     hbm = pl.BlockSpec(memory_space=pl.ANY)
     adjoint, gain = pl.pallas_call(
@@ -691,7 +799,7 @@
             jax.ShapeDtypeStruct((ROWS, D), F32),
             jax.ShapeDtypeStruct((1, D), F32),
         ),
-        in_specs=[vmem] * 5 + [hbm] * 4,
+        in_specs=[hbm] * 9,
         out_specs=(vmem, vmem),
         scratch_shapes=scratch(),
         compiler_params=pltpu.CompilerParams(

time: 127 us -> 120 us (0.945)
  Pallas kernels: 122 us -> 116 us
    pallas_call x1, Pallas kernels: 122 us -> 116 us  [body(): pl.pallas_call(kernel, out_shape=(jax.ShapeDtypeStruct((ROWS, D), F32), j...]
where the time goes in v3:
time: 120 us
  Pallas kernels  116 us (97%)
  local copies, waits for them, and re-layouts  2.89 us (2%)
    pallas_call x1, Pallas kernels, body(): pl.pallas_call(kernel, out_shape=(jax.ShapeDtypeStruct((ROWS, D), F32), j...  116 us
    unnamed x2, local copies, waits for them, and re-layouts  2.89 us

profile of v3, /device:TPU:1, one launch (start us, length us, event | category | flops | bytes accessed | tf_op | source)
XLA Modules:
  0.0 119.8 jit_solution(17058390000075559669)
XLA Ops:
  0.6 116.3 %deq_backward.1 = (f32[8,4096]{1,0:T(8,128)}, f32[1,4096]{1,0:T(1,128)}) custom-call(bf16[8,4096]{1,0:T(8,128)(2,1)} %point_hbm.1, bf16[8,4096]{1,0:T(8,128)(2,1)} %inc_hbm.1, f32[1,4096]{1,0:T(1,128)} %bitcast.2, f32[1,128]{1,0:T(1,128)} %constant.5.freq_hbm, s32[32,32]{1,0:T(8,128)} %lay_hbm.1, bf16[4096,256]{1,0:T(8,128)(2,1)} %wq_hbm.1, ...), custom_call_target="tpu_custom_call" | custom-call | tf_op jit(solution)/shard_map/deq_backward/pallas_call | solution.py:796
  116.9 1.6 %copy.13 = f32[8,4096]{1,0:T(8,128)} copy(f32[8,4096]{1,0:T(8,128)} %get-tuple-element.8) | data formatting | bytes 262144
  118.5 1.3 %copy.14 = f32[4096]{0:T(1024)} copy(f32[4096]{0:T(1024)} %bitcast.3) | data formatting | bytes 32768

commit v4 on v3

--- a/solution.py
+++ b/solution.py
@@ -54,7 +54,7 @@
     adj_ref, gg_ref,
     point_ref, inc_ref, gain_ref, freq_ref, lay_ref,
     wqkv, wo, wqkv_t, wo_t, cosb, sinb, loc, sc16, in16, ir16, irl, agx, agi, agc,
-    kb, vb, qb, gb, oa, ob, ga2, gb2, oa2, ob2, st, bq, bk, pq, pk, att, dqkv,
+    gpk, kb, vb, qb, gb, oa, ob, ga2, gb2, oa2, ob2, st, bq, bk, pq, pk, att, dqkv,
     tot, drv, rsrc, rrv, pair, gn, inl, inr, adj16, adjr, gacc, gt, gs, gh,
     in_sem, w_sem, ags, agr, fws, fwr, d2s, d2r, rgs, rgr, yxs, yxr, yfs, yfr, sts, str_,
     gvs, gvr, rss, rsr, gts, gtr, gss, gsr,
@@ -110,8 +110,6 @@
         for i, h in enumerate((wq_hbm, wk_hbm, wv_hbm))
     ]
     loads.append(pltpu.make_async_copy(wo_hbm, wo, w_sem.at[3]))
-    for cp in loads:
-        cp.start()
 
     @pl.loop(0, NZ)
     def _(i):
@@ -133,6 +131,8 @@
 
     for cp in small:
         cp.wait()
+    for cp in loads:
+        cp.start()
     pt = point_ref[...].astype(F32)
     inv = lax.rsqrt(jnp.mean(pt * pt, axis=1, keepdims=True) + EPS)
     loc[0] = pt * inv
@@ -157,42 +157,32 @@
     remote(loc.at[1, :, far_half], in16.at[far_rows, :], d2s.at[1], d2r.at[1], partner).wait_recv()
     remote(irl, ir16.at[far_rows, :], d2s.at[2], d2r.at[2], partner).wait_recv()
 
-    def gather_sends(buf, g):
+    def gather_start(buf, g):
         mine = buf.at[chip, :, own_half]
-        out = [remote(mine, mine, ags.at[g, 7], agr.at[g, 7], partner)]
+        remote(mine, mine, fws.at[g], fwr.at[g], partner).start()
         for k in range(7):
             a, b = chip_to(k)
-            out.append(remote(mine, mine, ags.at[g, k], agr.at[g, k], dev(yh_=a, x_=b)))
-        return out
-
-    def gather_start(buf, g):
-        for cp in gather_sends(buf, g):
-            cp.start()
+            remote(mine, mine, ags.at[g], agr.at[g, k], dev(yh_=a, x_=b)).start()
 
     def gather_pass(buf, g):
         for k in range(7):
             slot = buf.at[chip_from(k), :, own_half]
-            remote(slot, slot, ags.at[g, k], agr.at[g, k], partner).wait_recv()
-            remote(slot, slot, fws.at[g, k], fwr.at[g, k], partner).start()
+            remote(slot, slot, ags.at[g], agr.at[g, k], partner).wait_recv()
+            remote(slot, slot, fws.at[g], fwr.at[g], partner).start()
 
     def gather_finish(buf, g):
-        far = buf.at[chip, :, far_half]
-        remote(far, far, ags.at[g, 7], agr.at[g, 7], partner).wait_recv()
-        for k in range(7):
-            far = buf.at[chip_from(k), :, far_half]
-            remote(far, far, fws.at[g, k], fwr.at[g, k], partner).wait_recv()
+        far = buf.at[:, :, far_half]
+        remote(far, far, fws.at[g], fwr.at[g], partner).wait_recv()
 
     def gather_sent(buf, g):
-        for k in range(7):
-            slot = buf.at[chip_from(k), :, own_half]
-            remote(slot, slot, fws.at[g, k], fwr.at[g, k], partner).wait_send()
-        for cp in gather_sends(buf, g):
-            cp.wait_send()
+        own = buf.at[:, :, own_half]
+        remote(own, own, fws.at[g], fwr.at[g], partner).wait_send()
+        seven = buf.at[pl.ds(0, 7), :, own_half]
+        remote(seven, seven, ags.at[g], agr.at[g, 0], partner).wait_send()
 
     agx[chip, :, own_half] = (gain_half * sc16[...]).astype(BF16)
     gather_start(agx, 0)
     agi[chip, :, own_half] = in16[...].astype(BF16)
-    gather_start(agi, 1)
 
     row_tok = s * TOK + lax.broadcasted_iota(jnp.int32, (TOK, 1), 0)
     row_blk = row_tok // BLK
@@ -232,6 +222,7 @@
         wqkv_t[:, rows] = jnp.transpose(wqkv[rows, :])
         wo_t[rows, :] = jnp.transpose(wo[:, rows])
 
+    gather_start(agi, 1)
     gather_pass(agx, 0)
     gather_finish(agx, 0)
 
@@ -255,6 +246,7 @@
         return near & some
 
     bufs = (kb, vb, qb, gb, oa, ga2, gb2, oa2)
+    slot_of = {GA: K, GB: V, OA2: OA}
 
     def hop(stream, sgn, d, at):
         block = bufs[stream].at[lax.rem(at - sgn * (d - 1) + NZ, NZ)]
@@ -272,8 +264,14 @@
     def over(stream, origin):
         dst, n = (ob2, 1) if stream == GB else (ob, 0)
         return remote(
-            bufs[stream].at[origin], dst.at[origin], yfs.at[n, origin], yfr.at[n, origin], across
+            bufs[stream].at[origin], dst.at[origin], yfs.at[n], yfr.at[n], across
         )
+
+    def over_sent(stream):
+        @pl.when(yl == (0 if stream == V else 1))
+        def _():
+            n = 1 if stream == GB else 0
+            remote(bufs[stream], ob2 if n else ob, yfs.at[n], yfr.at[n], across).wait_send()
 
     def send_over(stream, origin):
         @pl.when(yl == (0 if stream == V else 1))
@@ -309,17 +307,12 @@
                     def _():
                         hop(stream, sgn, d, z).wait_send()
 
-            if stream in (V, G, GB):
-
-                @pl.when(yl == (0 if stream == V else 1))
-                def _():
-                    for i in range(NZ):
-                        over(stream, i).wait_send()
+            if stream in (V, G):
+                over_sent(stream)
 
     def over_wait(n):
         buf = ob2 if n else ob
-        for i in range(NZ):
-            remote(buf.at[i], buf.at[i], yfs.at[n, i], yfr.at[n, i], across).wait_recv()
+        remote(buf, buf, yfs.at[n], yfr.at[n], across).wait_recv()
 
     def wanted2(stream, sgn, d, at):
         full = depth(sgn)
@@ -341,7 +334,8 @@
         block = bufs[stream].at[origin]
         z_to = lax.rem(z + sgn * step + NZ, NZ)
         i = 0 if sgn > 0 else 1
-        sems = rgs.at[stream, i, d - 1], rgr.at[stream, i, d - 1]
+        n = slot_of[stream]
+        sems = rgs.at[n, i, d - 1], rgr.at[n, i, d - 1]
         if stream == OA2 and d == 2:
             return remote(ga2.at[origin], block, *sems, dev(yl_=1 - yl, z_=z_to))
         return remote(block, block, *sems, dev(z_=z_to))
@@ -388,11 +382,7 @@
                         far_hop(stream, sgn, d, z).wait_send()
 
             if stream == GB:
-
-                @pl.when(yl == 1)
-                def _():
-                    for i in range(NZ):
-                        over(stream, i).wait_send()
+                over_sent(stream)
 
     def cross(src, dst, i):
         return remote(src.at[z], dst.at[z], yxs.at[i], yxr.at[i], across)
@@ -491,18 +481,15 @@
     def _():
         forward(((kb, vb), (oa, ob)))
 
-    def stats_sends(it):
-        out = []
+    def stats_start(it):
+        mine = st.at[it, s]
         for k in range(len(SEQ_STEPS)):
             a, b = seq_to(k)
-            mine = st.at[it, s]
-            out.append(remote(mine, mine, sts.at[it, k], str_.at[it, k], dev(yl_=a, z_=b)))
-        return out
-
-    def stats_wait(it):
-        for k in range(len(SEQ_STEPS)):
-            slot = st.at[it, seq_from(k)]
-            remote(slot, slot, sts.at[it, k], str_.at[it, k], partner).wait_recv()
+            remote(mine, mine, sts.at[it], str_.at[it], dev(yl_=a, z_=b)).start()
+
+    def stats_all(it):
+        most = st.at[it, pl.ds(0, len(SEQ_STEPS))]
+        return remote(most, most, sts.at[it], str_.at[it], partner)
 
     def own_grad(it, h):
         return gb[z, :, lanes(h)] if it == 0 else (ga2, gb2)[h][z]
@@ -521,10 +508,19 @@
                 out = o if out is None else out + o
             dqkv[:, lanes(h)] = turn(out * scale, True).astype(BF16)
 
+    def key_scores(it, parts):
+        for h in range(HEADS_DEV):
+            for i, (queries, grads, late) in enumerate(parts):
+                if it == 0:
+                    query = rows_of(queries, h)
+                    pk[h, i] = dot(kb[z, :, lanes(h)], query, NT) * scale + bk[i]
+                    grad = rows_of(grads, h)
+                else:
+                    grad = late[h][...].reshape(PLANE, HEAD_DIM)
+                gpk[h, i] = dot(vb[z, :, lanes(h)], grad, NT)
+
     def key_side(it, parts, planes):
         for h in range(HEADS_DEV):
-            key = kb[z, :, lanes(h)]
-            value = vb[z, :, lanes(h)]
             gk, gv = None, None
             for i, (queries, grads, late) in enumerate(parts):
                 row = lambda n, r: jnp.concatenate(
@@ -532,7 +528,7 @@
                 )
                 query = rows_of(queries, h)
                 if it == 0:
-                    p = jnp.exp(dot(key, query, NT) * scale + bk[i] - row(0, h))
+                    p = jnp.exp(pk[h, i] - row(0, h))
                     pk[h, i] = p
                     grad = rows_of(grads, h)
                 else:
@@ -540,8 +536,7 @@
                     grad = late[h][...].reshape(PLANE, HEAD_DIM)
                 v = dot(p.astype(BF16), grad)
                 gv = v if gv is None else gv + v
-                gp = dot(value, grad, NT)
-                gsc = (p * (gp - row(it, 2 + h))).astype(BF16)
+                gsc = (p * (gpk[h, i] - row(it, 2 + h))).astype(BF16)
                 k = dot(gsc, query)
                 gk = k if gk is None else gk + k
             dqkv[:, lanes(HEADS_DEV + h)] = turn(gk * scale, True).astype(BF16)
@@ -556,20 +551,33 @@
         def _():
             query_side(it, ((kb, vb), (oa, ob)))
 
+    most = gs.at[pl.ds(0, len(SEQ_STEPS))]
+    gain_seq = remote(most, most, gss.at[0], gsr.at[0], partner)
+    most = gt.at[pl.ds(0, 7)]
+    gain_chip = remote(most, most, gts.at[0], gtr.at[0], partner)
+
     def backward(it):
-        stats_wait(it)
+        own = (qb, gb, (ga2, gb2))
+        other = (oa, ob, (oa2, ob2))
 
         @pl.when(yl == 0)
         def _():
             over_wait(it)
+            key_scores(it, (own, other))
+
+        @pl.when(yl == 1)
+        def _():
+            key_scores(it, (own,))
+
+        stats_all(it).wait_recv()
 
         @pl.when(yl == 0)
         def _():
-            key_side(it, ((qb, gb, (ga2, gb2)), (oa, ob, (oa2, ob2))), (yl, 1 - yl))
+            key_side(it, (own, other), (yl, 1 - yl))
 
         @pl.when(yl == 1)
         def _():
-            key_side(it, ((qb, gb, (ga2, gb2)),), (yl,))
+            key_side(it, (own,), (yl,))
 
         wide = HALF // CHUNKS
         gives = []
@@ -589,12 +597,13 @@
             for k in range(7):
                 a, b = chip_to(k)
                 rsrc[it, j, k] = pair[j, a * NX + b].astype(BF16)
-                cp = remote(
-                    rsrc.at[it, j, k], rrv.at[it, j, k], rss.at[it, j, k], rsr.at[it, j, k],
+                remote(
+                    rsrc.at[it, j, k], rrv.at[it, j, k], rss.at[it, j], rsr.at[it, j],
                     dev(yh_=a, x_=b),
-                )
-                cp.start()
-                sends.append(cp)
+                ).start()
+            sends.append(
+                remote(rsrc.at[it, j], rrv.at[it, j], rss.at[it, j], rsr.at[it, j], partner)
+            )
 
         for j in range(CHUNKS):
             gives[j].wait_recv()
@@ -611,25 +620,29 @@
             gn[:, here] = pair[j, chip]
         if last_term:
             gs[s] = gacc[...]
-            for cp in gain_seq_sends():
-                cp.start()
+            for k in range(len(SEQ_STEPS)):
+                a, b = seq_to(k)
+                remote(gs.at[s], gs.at[s], gss.at[0], gsr.at[0], dev(yl_=a, z_=b)).start()
             for j in range(CHUNKS):
                 scatter(j)
-            for k in range(len(SEQ_STEPS)):
-                slot = gs.at[seq_from(k)]
-                remote(slot, slot, gss.at[k], gsr.at[k], partner).wait_recv()
+            gain_seq.wait_recv()
             acc = gs[0]
             for i in range(1, NY * NZ):
                 acc = acc + gs[i]
             gt[chip] = acc
-            for cp in gain_chip_sends():
-                cp.start()
-            sent.extend(gain_seq_sends() + gain_chip_sends())
+            for k in range(7):
+                a, b = chip_to(k)
+                remote(
+                    gt.at[chip], gt.at[chip], gts.at[0], gtr.at[0], dev(yh_=a, x_=b)
+                ).start()
+            sent.extend([gain_seq, gain_chip])
         for j in range(CHUNKS):
             here = pl.ds(j * wide, wide)
+            sends[j].wait_recv()
+            total = gn[:, here]
             for k in range(7):
-                sends[7 * j + k].wait_recv()
-                gn[:, here] += rrv[it, j, k].astype(F32)
+                total = total + rrv[it, j, k].astype(F32)
+            gn[:, here] = total
 
         grad_normed = gn[...]
         scaled = sc16[...]
@@ -648,28 +661,12 @@
             gather_start(agc, 2)
         sent.extend(gives + [share] + sends)
 
-    def gain_chip_sends():
-        out = []
-        for k in range(7):
-            a, b = chip_to(k)
-            out.append(
-                remote(gt.at[chip], gt.at[chip], gts.at[k], gtr.at[k], dev(yh_=a, x_=b))
-            )
-        return out
-
-    def gain_seq_sends():
-        out = []
-        for k in range(len(SEQ_STEPS)):
-            a, b = seq_to(k)
-            out.append(remote(gs.at[s], gs.at[s], gss.at[k], gsr.at[k], dev(yl_=a, z_=b)))
-        return out
-
-    for cp in stats_sends(0):
-        cp.start()
+    stats_start(0)
     ring_step(4, Q, G)
     own_queries(0)
     backward(0)
 
+    ring_sent(K, V, Q, G, OA)
     gather_pass(agc, 2)
     gather_finish(agc, 2)
     grad2 = dot(agc[...].reshape(TOK, D), wo_t[...]).astype(BF16)
@@ -693,8 +690,7 @@
                 own_grad(1, h).astype(F32) * att[:, lanes(h)].astype(F32), axis=1, keepdims=True
             )
         )
-    for cp in stats_sends(1):
-        cp.start()
+    stats_start(1)
     own_queries(1)
     far_take(GB, 2)
     far_take(OA2, 2)
@@ -715,9 +711,7 @@
     back = remote(adj16.at[far_rows, :], adjr, d2s.at[7], d2r.at[7], partner)
     back.start()
     adj_ref[:, own_half] = adj16[own_rows, :]
-    for k in range(7):
-        slot = gt.at[chip_from(k)]
-        remote(slot, slot, gts.at[k], gtr.at[k], partner).wait_recv()
+    gain_chip.wait_recv()
     acc = gt[0]
     for i in range(1, CHIPS):
         acc = acc + gt[i]
@@ -729,7 +723,6 @@
     gg_ref[:, own_half] = gh[0]
     last.wait_recv()
     gg_ref[:, far_half] = gh[1]
-    ring_sent(K, V, Q, G, OA)
     far_sent(GA, GB, OA2)
     gather_sent(agx, 0)
     gather_sent(agi, 1)
@@ -747,7 +740,7 @@
     def _():
         cross(ga2, oa2, 1).wait_send()
 
-    for cp in sent + stats_sends(0) + stats_sends(1) + [back, last]:
+    for cp in sent + [stats_all(0), stats_all(1), back, last]:
         cp.wait_send()
 
 
@@ -765,6 +758,7 @@
         v((2, ROWS, D), F32), v((CROWS, HALF), F32), v((CROWS, HALF), F32), v((CROWS, 128), F32),
         v((ROWS, 128), F32),
         v((CHIPS, CROWS, D), BF16), v((CHIPS, CROWS, D), BF16), v((CHIPS, CROWS, D), BF16),
+        v((HEADS_DEV, 2, TOK, PLANE), F32),
         v(block, BF16), v(block, BF16), v(block, BF16), v(block, BF16), v(block, BF16),
         v(block, BF16),
         v(half_block, BF16), v(half_block, BF16), v(half_block, BF16), v(half_block, BF16),
@@ -778,11 +772,11 @@
         v((ITERS, CROWS, 128), F32), v((ITERS, CROWS, 128), F32),
         v((CROWS, HALF), F32), v((ROWS, HALF), F32), v((1, HALF), F32),
         v((CHIPS, 1, HALF), F32), v((NY * NZ, 1, HALF), F32), v((2, 1, HALF), F32),
-        dma((5,)), dma((4,)), dma((3, 8)), dma((3, 8)), dma((3, 7)), dma((3, 7)), dma((9,)), dma((9,)),
-        dma((8, 2, 4)), dma((8, 2, 4)), dma((2,)), dma((2,)), dma((2, NZ)), dma((2, NZ)),
-        dma((ITERS, 15)), dma((ITERS, 15)), dma((ITERS, CHUNKS)), dma((ITERS, CHUNKS)),
-        dma((ITERS, CHUNKS, 7)), dma((ITERS, CHUNKS, 7)),
-        dma((7,)), dma((7,)), dma((15,)), dma((15,)),
+        dma((5,)), dma((4,)), dma((3,)), dma((3, 7)), dma((3,)), dma((3,)), dma((9,)), dma((9,)),
+        dma((5, 2, 4)), dma((5, 2, 4)), dma((2,)), dma((2,)), dma((2,)), dma((2,)),
+        dma((ITERS,)), dma((ITERS,)), dma((ITERS, CHUNKS)), dma((ITERS, CHUNKS)),
+        dma((ITERS, CHUNKS)), dma((ITERS, CHUNKS)),
+        dma((1,)), dma((1,)), dma((1,)), dma((1,)),
     ]
 
 

time: 120 us -> 117 us (0.975)
  Pallas kernels: 116 us -> 113 us
    pallas_call x1, Pallas kernels: 116 us -> 113 us  [body(): pl.pallas_call(kernel, out_shape=(jax.ShapeDtypeStruct((ROWS, D), F32), j...]
where the time goes in v4:
time: 117 us; the launch traced here: 116 us
  Pallas kernels  113 us (97%)
  local copies, waits for them, and re-layouts  2.89 us (2%)
    pallas_call x1, Pallas kernels, body(): pl.pallas_call(kernel, out_shape=(jax.ShapeDtypeStruct((ROWS, D), F32), j...  113 us
    unnamed x2, local copies, waits for them, and re-layouts  2.89 us

profile of v4, /device:TPU:1, one launch (start us, length us, event | category | flops | bytes accessed | tf_op | source)
XLA Modules:
  0.0 116.5 jit_solution(506883544238185897)
XLA Ops:
  0.6 113.0 %deq_backward.1 = (f32[8,4096]{1,0:T(8,128)}, f32[1,4096]{1,0:T(1,128)}) custom-call(bf16[8,4096]{1,0:T(8,128)(2,1)} %point_hbm.1, bf16[8,4096]{1,0:T(8,128)(2,1)} %inc_hbm.1, f32[1,4096]{1,0:T(1,128)} %bitcast.2, f32[1,128]{1,0:T(1,128)} %constant.5.freq_hbm, s32[32,32]{1,0:T(8,128)} %lay_hbm.1, bf16[4096,256]{1,0:T(8,128)(2,1)} %wq_hbm.1, ...), custom_call_target="tpu_custom_call" | custom-call | tf_op jit(solution)/shard_map/deq_backward/pallas_call | solution.py:790
  113.6 1.6 %copy.13 = f32[8,4096]{1,0:T(8,128)} copy(f32[8,4096]{1,0:T(8,128)} %get-tuple-element.8) | data formatting | bytes 262144
  115.2 1.3 %copy.14 = f32[4096]{0:T(1024)} copy(f32[4096]{0:T(1024)} %bitcast.3) | data formatting | bytes 32768

commit v5 on v4

--- a/solution.py
+++ b/solution.py
@@ -56,7 +56,7 @@
     wqkv, wo, wqkv_t, wo_t, cosb, sinb, loc, sc16, in16, ir16, irl, agx, agi, agc,
     gpk, kb, vb, qb, gb, oa, ob, ga2, gb2, oa2, ob2, st, bq, bk, pq, pk, att, dqkv,
     tot, drv, rsrc, rrv, pair, gn, inl, inr, adj16, adjr, gacc, gt, gs, gh,
-    in_sem, w_sem, ags, agr, fws, fwr, d2s, d2r, rgs, rgr, yxs, yxr, yfs, yfr, sts, str_,
+    out_sem, in_sem, w_sem, ags, agr, fws, fwr, d2s, d2r, rgs, rgr, yxs, yxr, yfs, yfr, sts, str_,
     gvs, gvr, rss, rsr, gts, gtr, gss, gsr,
 ):
     yl, z, yh, x, c = (lax.axis_index(a) for a in AXES)
@@ -421,15 +421,21 @@
     gb[z] = dot(agi[...].reshape(TOK, D), wo_t[...]).astype(BF16)
     ring_start(G)
     ring_step(1, OA)
-    ring_step(2, K, V)
+    ring_step(2, K)
+    ring_step(2, V)
+    ring_step(1, G)
+    ring_step(1, Q)
     ring_step(2, OA)
-    ring_step(1, Q, G)
-    ring_step(3, K, V)
+    ring_step(3, K)
+    ring_step(3, V)
+    ring_step(2, G)
+    ring_step(2, Q)
     ring_step(3, OA)
-    ring_step(2, Q, G)
-    ring_step(4, K, V)
+    ring_step(4, K)
+    ring_step(4, V)
+    ring_step(3, G)
+    ring_step(3, Q)
     ring_step(4, OA)
-    ring_step(3, Q, G)
     @pl.when(yl == 1)
     def _():
         over_wait(0)
@@ -710,7 +716,8 @@
 
     back = remote(adj16.at[far_rows, :], adjr, d2s.at[7], d2r.at[7], partner)
     back.start()
-    adj_ref[:, own_half] = adj16[own_rows, :]
+    outs = [pltpu.make_async_copy(adj16.at[own_rows, :], adj_ref.at[:, own_half], out_sem.at[0])]
+    outs[0].start()
     gain_chip.wait_recv()
     acc = gt[0]
     for i in range(1, CHIPS):
@@ -719,10 +726,13 @@
     last = remote(gh.at[0], gh.at[1], d2s.at[8], d2r.at[8], partner)
     last.start()
     back.wait_recv()
-    adj_ref[:, far_half] = adjr[...]
-    gg_ref[:, own_half] = gh[0]
+    outs.append(pltpu.make_async_copy(adjr, adj_ref.at[:, far_half], out_sem.at[1]))
+    outs[1].start()
+    outs.append(pltpu.make_async_copy(gh.at[0], gg_ref.at[:, own_half], out_sem.at[2]))
+    outs[2].start()
     last.wait_recv()
-    gg_ref[:, far_half] = gh[1]
+    outs.append(pltpu.make_async_copy(gh.at[1], gg_ref.at[:, far_half], out_sem.at[3]))
+    outs[3].start()
     far_sent(GA, GB, OA2)
     gather_sent(agx, 0)
     gather_sent(agi, 1)
@@ -742,6 +752,8 @@
 
     for cp in sent + [stats_all(0), stats_all(1), back, last]:
         cp.wait_send()
+    for cp in outs:
+        cp.wait()
 
 
 def scratch():
@@ -772,12 +784,17 @@
         v((ITERS, CROWS, 128), F32), v((ITERS, CROWS, 128), F32),
         v((CROWS, HALF), F32), v((ROWS, HALF), F32), v((1, HALF), F32),
         v((CHIPS, 1, HALF), F32), v((NY * NZ, 1, HALF), F32), v((2, 1, HALF), F32),
-        dma((5,)), dma((4,)), dma((3,)), dma((3, 7)), dma((3,)), dma((3,)), dma((9,)), dma((9,)),
+        dma((4,)), dma((5,)), dma((4,)), dma((3,)), dma((3, 7)), dma((3,)), dma((3,)), dma((9,)), dma((9,)),
         dma((5, 2, 4)), dma((5, 2, 4)), dma((2,)), dma((2,)), dma((2,)), dma((2,)),
         dma((ITERS,)), dma((ITERS,)), dma((ITERS, CHUNKS)), dma((ITERS, CHUNKS)),
         dma((ITERS, CHUNKS)), dma((ITERS, CHUNKS)),
         dma((1,)), dma((1,)), dma((1,)), dma((1,)),
     ]
+
+
+def hand_over(a_ref, g_ref, a_out, g_out):
+    a_out[...] = a_ref[...]
+    g_out[...] = g_ref[...]
 
 
 def body(
@@ -794,7 +811,7 @@
             jax.ShapeDtypeStruct((1, D), F32),
         ),
         in_specs=[hbm] * 9,
-        out_specs=(vmem, vmem),
+        out_specs=(hbm, hbm),
         scratch_shapes=scratch(),
         compiler_params=pltpu.CompilerParams(
             collective_id=0, has_side_effects=True, vmem_limit_bytes=62 * 1024 * 1024
@@ -804,6 +821,16 @@
         fixed_point, incoming, norm_gain[None, :], freq[None, :], layout,
         query_weight, key_weight, value_weight, out_weight,
     )
+    adjoint, gain = pl.pallas_call(
+        hand_over,
+        out_shape=(
+            jax.ShapeDtypeStruct((ROWS, D), F32),
+            jax.ShapeDtypeStruct((1, D), F32),
+        ),
+        in_specs=[vmem] * 2,
+        out_specs=(vmem, vmem),
+        name="hand_over",
+    )(adjoint, gain)
     return adjoint, gain[0]
 
 

time: 117 us -> 114 us (0.974)
  local copies, waits for them, and re-layouts: 2.89 us -> 0 us
    unnamed x2 -> x0, local copies, waits for them, and re-layouts: 2.89 us -> none
    pallas_call x0 -> x1, Pallas kernels: none -> 1.57 us  [body(): pl.pallas_call(hand_over, out_shape=(jax.ShapeDtypeStruct((ROWS, D), F32)...]
    pallas_call x1, Pallas kernels: 113 us -> 112 us  [body(): pl.pallas_call(kernel, out_shape=(jax.ShapeDtypeStruct((ROWS, D), F32), j...]
where the time goes in v5:
time: 114 us
  Pallas kernels  113 us (99%)
    pallas_call x1, Pallas kernels, body(): pl.pallas_call(kernel, out_shape=(jax.ShapeDtypeStruct((ROWS, D), F32), j...  112 us

profile of v5, /device:TPU:1, one launch (start us, length us, event | category | flops | bytes accessed | tf_op | source)
XLA Modules:
  0.0 113.9 jit_solution(16275891289518202388)
XLA Ops:
  0.6 111.7 %deq_backward.1 = (f32[8,4096]{1,0:T(8,128)}, f32[1,4096]{1,0:T(1,128)}) custom-call(bf16[8,4096]{1,0:T(8,128)(2,1)} %point_hbm.1, bf16[8,4096]{1,0:T(8,128)(2,1)} %inc_hbm.1, f32[1,4096]{1,0:T(1,128)} %bitcast.2, f32[1,128]{1,0:T(1,128)} %constant.5.freq_hbm, s32[32,32]{1,0:T(8,128)} %lay_hbm.1, bf16[4096,256]{1,0:T(8,128)(2,1)} %wq_hbm.1, ...), custom_call_target="tpu_custom_call" | custom-call | tf_op jit(solution)/shard_map/deq_backward/pallas_call | solution.py:807
  112.3 1.6 %hand_over.1 = (f32[8,4096]{1,0:T(8,128)}, f32[1,4096]{1,0:T(1,128)}) custom-call(f32[8,4096]{1,0:T(8,128)} %get-tuple-element.6.a_ref, f32[1,4096]{1,0:T(1,128)} %get-tuple-element.7.g_ref), custom_call_target="tpu_custom_call" | custom-call | tf_op jit(solution)/shard_map/hand_over/pallas_call | solution.py:824

commit v6 on v5

--- a/solution.py
+++ b/solution.py
@@ -679,16 +679,16 @@
     ga2[z] = grad2[:, :HEAD_DIM]
     gb2[z] = grad2[:, HEAD_DIM:]
 
-    far_send(OA2, 2)
     far_send(GB, 2)
-
-    @pl.when(yl == 1)
-    def _():
-        cross(ga2, oa2, 1).start()
-
-    far_send(GA, 2)
     far_send(GB, 1)
     send_over(GB, z)
+    far_send(OA2, 2)
+
+    @pl.when(yl == 1)
+    def _():
+        cross(ga2, oa2, 1).start()
+
+    far_send(GA, 2)
     far_send(GA, 1)
     for h in range(HEADS_DEV):
         st[1, s, pl.ds(2 + h, 1), :] = as_row(

time: 114 us -> 114 us (level)
  no operation moved by 1% of the time
where the time goes in v6:
time: 114 us
  Pallas kernels  113 us (99%)
    pallas_call x1, Pallas kernels, body(): pl.pallas_call(kernel, out_shape=(jax.ShapeDtypeStruct((ROWS, D), F32), j...  112 us

profile of v6, /device:TPU:1, one launch (start us, length us, event | category | flops | bytes accessed | tf_op | source)
XLA Modules:
  0.0 113.8 jit_solution(2957440083190935039)
XLA Ops:
  0.6 111.6 %deq_backward.1 = (f32[8,4096]{1,0:T(8,128)}, f32[1,4096]{1,0:T(1,128)}) custom-call(bf16[8,4096]{1,0:T(8,128)(2,1)} %point_hbm.1, bf16[8,4096]{1,0:T(8,128)(2,1)} %inc_hbm.1, f32[1,4096]{1,0:T(1,128)} %bitcast.2, f32[1,128]{1,0:T(1,128)} %constant.5.freq_hbm, s32[32,32]{1,0:T(8,128)} %lay_hbm.1, bf16[4096,256]{1,0:T(8,128)(2,1)} %wq_hbm.1, ...), custom_call_target="tpu_custom_call" | custom-call | tf_op jit(solution)/shard_map/deq_backward/pallas_call | solution.py:807
  112.3 1.6 %hand_over.1 = (f32[8,4096]{1,0:T(8,128)}, f32[1,4096]{1,0:T(1,128)}) custom-call(f32[8,4096]{1,0:T(8,128)} %get-tuple-element.6.a_ref, f32[1,4096]{1,0:T(1,128)} %get-tuple-element.7.g_ref), custom_call_target="tpu_custom_call" | custom-call | tf_op jit(solution)/shard_map/hand_over/pallas_call | solution.py:824
